TPU v7x, 256 devices: a whole 4x4x8 slice. The times are simulated.
256 devices in a mesh: col: 32 (over z, y), row: 8 (over x, core).
Axes of the slice: x: 4, y: 4, z: 8, core: 2. Of those that a mesh axis runs over, the one named last changes fastest.
Arguments:
- mask: int32 [32768, 8192], P('row', 'col')
- user_emb: bfloat16 [32768, 256], P(('row', 'col'))
- item_emb: bfloat16 [8192, 256], P(('col', 'row'))
- queries: int32 [1024], replicated
Outputs:
- output 1: bfloat16 [32768, 256], P(('row', 'col'))
- output 2: bfloat16 [8192, 256], P(('col', 'row'))
- output 3: float32 [1024, 8192], P(None, ('col', 'row'))
All inputs are finite; a program needn't handle non-finite values.
Results may differ from a plain program's by a relative error of at most 0.00644127.
Values are sent between devices in bfloat16 or wider.
A program may use at most 768 MiB of HBM per device.

v0:
```python
import jax
import jax.numpy as jnp
from jax import lax
from jax.sharding import PartitionSpec as P

LAYERS = 3


def norm_block(mask_blk):
    deg_user = lax.psum(jnp.sum(mask_blk, axis=1), 'col')
    deg_item = lax.psum(jnp.sum(mask_blk, axis=0), 'row')
    inv_user = lax.rsqrt(jnp.maximum(deg_user, 1).astype(jnp.float32))
    inv_item = lax.rsqrt(jnp.maximum(deg_item, 1).astype(jnp.float32))
    return (inv_user[:, None] * mask_blk.astype(jnp.float32) * inv_item[None, :]).astype(jnp.bfloat16)


def query_scores(final_user, final_item, queries, shard_pos):
    rows_local = final_user.shape[0]
    local_idx = queries - shard_pos * rows_local
    owned = (local_idx >= 0) & (local_idx < rows_local)
    picked = jnp.take(final_user, jnp.clip(local_idx, 0, rows_local - 1), axis=0)
    picked = jnp.where(owned[:, None], picked, jnp.zeros_like(picked))
    picked = lax.psum(picked, ('row', 'col'))
    return lax.dot_general(picked, final_item, (((1,), (1,)), ((), ())), preferred_element_type=jnp.float32)


def solution(mesh):
    n_col = mesh.shape['col']
    contract_rows = (((0,), (0,)), ((), ()))

    def device_step(mask_blk, user_shard, item_shard, queries):
        norm_adj = norm_block(mask_blk)
        user_cur = user_shard
        item_cur = item_shard
        user_sum = user_shard.astype(jnp.float32)
        item_sum = item_shard.astype(jnp.float32)
        for layer_idx in range(LAYERS):
            item_panel = lax.all_gather(item_cur, 'row', axis=0, tiled=True)
            user_part = jnp.dot(norm_adj, item_panel, preferred_element_type=jnp.float32)
            user_next = lax.psum_scatter(user_part, 'col', scatter_dimension=0, tiled=True).astype(jnp.bfloat16)
            user_panel = lax.all_gather(user_cur, 'col', axis=0, tiled=True)
            item_part = lax.dot_general(norm_adj, user_panel, contract_rows, preferred_element_type=jnp.float32)
            item_next = lax.psum_scatter(item_part, 'row', scatter_dimension=0, tiled=True).astype(jnp.bfloat16)
            user_sum = user_sum + user_next.astype(jnp.float32)
            item_sum = item_sum + item_next.astype(jnp.float32)
            user_cur = user_next
            item_cur = item_next
        final_user = (user_sum / (LAYERS + 1)).astype(jnp.bfloat16)
        final_item = (item_sum / (LAYERS + 1)).astype(jnp.bfloat16)
        shard_pos = lax.axis_index('row') * n_col + lax.axis_index('col')
        scores = query_scores(final_user, final_item, queries, shard_pos)
        return final_user, final_item, scores

    return jax.shard_map(device_step, mesh=mesh, in_specs=(P('row', 'col'), P(('row', 'col'), None), P(('col', 'row'), None), P()), out_specs=(P(('row', 'col'), None), P(('col', 'row'), None), P(None, ('col', 'row'))), check_vma=False)
```

profile of v0, /device:TPU:1, one launch (start us, length us, event | category | flops | bytes accessed | tf_op | source)
XLA Modules:
  0.0 1389.2 jit_solution(9829516401373413536)
XLA Ops:
  7.2 0.0 all-gather.4.cloned.1.call-start
  7.2 0.7 all-gather.4.cloned.1.call-update
  7.9 0.0 reduce-scatter.9.cloned.1.call-start
  7.9 2.8 fusion.1
  10.8 8.5 psum.22
  19.3 118.6 %psum.21 = s32[4096]{0:T(1024)S(1)} all-reduce(s32[4096]{0:T(1024)S(1)} %get-tuple-element.3), channel_id=1, replica_groups=mesh['col'=32,'row'=8] {'col'}, use_global_device_ids=true, to_apply=%region_1.0 | all-reduce | flops 4096 | bytes 32768 | tf_op jit(solution)/shard_map/psum | solution.py:10
  137.9 2.6 multiply_convert_fusion
  140.5 0.0 copy-start.5
  140.5 0.0 all-gather.4.cloned.1.call-done
  140.5 3.0 fusion.3
  143.5 0.0 reduce-scatter.9.cloned.1.call-update
  143.6 0.0 reduce-scatter.7.cloned.1.call-start
  143.6 0.0 copy-done.5
  143.6 42.4 %all_gather.18 = bf16[256,256]{1,0:T(8,128)(2,1)S(1)} all-gather(bf16[32,256]{1,0:T(8,128)(2,1)S(1)} %copy-done.5), channel_id=1, replica_groups=mesh['col'=32,'row'=8] {'row'}, dimensions={0}, use_global_device_ids=true | all-gather | bytes 147456 | tf_op jit(solution)/shard_map/all_gather | solution.py:38
  186.0 2.6 fusion.2
  188.7 0.0 reduce-scatter.7.cloned.1.call-update
  188.7 0.0 reduce-scatter.11.cloned.1.call-start
  188.7 7.8 reduce-scatter.9.cloned.1.call-done
  196.6 0.8 convert_element_type.67
  197.3 15.4 %all_gather.20 = bf16[256,256]{1,0:T(8,128)(2,1)S(1)} all-gather(bf16[32,256]{1,0:T(8,128)(2,1)S(1)} %convert_element_type.67), channel_id=1, replica_groups=mesh['col'=32,'row'=8] {'row'}, dimensions={0}, use_global_device_ids=true | all-gather | bytes 147456 | tf_op jit(solution)/shard_map/all_gather | solution.py:38
  212.7 2.7 fusion.4
  215.4 0.0 reduce-scatter.11.cloned.1.call-update
  215.4 0.0 all-gather.6.cloned.1.call-start
  215.5 204.3 %reduce-scatter.7.cloned.1.call-done = f32[128,256]{1,0:T(8,128)} async-done(((f32[4096,256]{1,0:T(8,128)}), f32[128,256]{1,0:T(8,128)}) %reduce-scatter.7.cloned.1.call-update) | async-done | bytes 131088 | tf_op jit(solution)/shard_map/reduce_scatter | solution.py:40
  419.8 1.5 convert_element_type.65
  421.3 0.0 all-gather.6.cloned.1.call-update
  421.3 0.0 all-gather.8.cloned.1.call-start
  421.4 223.7 %reduce-scatter.11.cloned.1.call-done = f32[128,256]{1,0:T(8,128)} async-done(((f32[4096,256]{1,0:T(8,128)}), f32[128,256]{1,0:T(8,128)}) %reduce-scatter.11.cloned.1.call-update) | async-done | bytes 131088 | tf_op jit(solution)/shard_map/reduce_scatter | solution.py:40
  645.0 1.5 convert_element_type.68
  646.6 0.0 all-gather.8.cloned.1.call-update
  646.6 0.0 reduce-scatter.13.cloned.1.call-start
  646.7 77.8 %all-gather.6.cloned.1.call-done = bf16[4096,256]{1,0:T(8,128)(2,1)} async-done(((bf16[128,256]{1,0:T(8,128)(2,1)}), bf16[4096,256]{1,0:T(8,128)(2,1)}) %all-gather.6.cloned.1.call-update) | async-done | bytes 2097168 | tf_op jit(solution)/shard_map/all_gather | solution.py:41
  724.4 3.0 fusion.5
  727.5 0.0 reduce-scatter.13.cloned.1.call-update
  727.5 0.0 copy-start.4
  727.5 0.0 reduce-scatter.17.cloned.1.call-start
  727.6 74.9 %all-gather.8.cloned.1.call-done = bf16[4096,256]{1,0:T(8,128)(2,1)} async-done(((bf16[128,256]{1,0:T(8,128)(2,1)}), bf16[4096,256]{1,0:T(8,128)(2,1)}) %all-gather.8.cloned.1.call-update) | async-done | bytes 2097168 | tf_op jit(solution)/shard_map/all_gather | solution.py:41
  802.5 3.0 fusion.7
  805.5 0.0 reduce-scatter.17.cloned.1.call-update
  805.6 0.0 reduce-scatter.15.cloned.1.call-start
  805.6 32.7 %reduce-scatter.13.cloned.1.call-done = f32[32,256]{1,0:T(8,128)} async-done(((f32[256,256]{1,0:T(8,128)}), f32[32,256]{1,0:T(8,128)}) %reduce-scatter.13.cloned.1.call-update) | async-done | bytes 32784 | tf_op jit(solution)/shard_map/reduce_scatter | solution.py:43
  838.3 34.8 %reduce-scatter.17.cloned.1.call-done = f32[32,256]{1,0:T(8,128)} async-done(((f32[256,256]{1,0:T(8,128)}), f32[32,256]{1,0:T(8,128)}) %reduce-scatter.17.cloned.1.call-update) | async-done | bytes 32784 | tf_op jit(solution)/shard_map/reduce_scatter | solution.py:43
  873.1 0.0 copy-done.4
  873.1 0.8 multiply_convert_fusion.2
  873.9 0.0 copy-start.6
  873.9 15.4 %all_gather.22 = bf16[256,256]{1,0:T(8,128)(2,1)S(1)} all-gather(bf16[32,256]{1,0:T(8,128)(2,1)S(1)} %get-tuple-element.6), channel_id=1, replica_groups=mesh['col'=32,'row'=8] {'row'}, dimensions={0}, use_global_device_ids=true | all-gather | bytes 147456 | tf_op jit(solution)/shard_map/all_gather | solution.py:38
  889.3 2.6 fusion.6
  891.9 0.0 copy-start.7
  891.9 0.0 reduce-scatter.15.cloned.1.call-update
  891.9 0.0 all-reduce.2.cloned.1.call-start
  892.0 0.6 copy-done.7
  892.6 217.2 %reduce-scatter.15.cloned.1.call-done = f32[128,256]{1,0:T(8,128)} async-done(((f32[4096,256]{1,0:T(8,128)}), f32[128,256]{1,0:T(8,128)}) %reduce-scatter.15.cloned.1.call-update) | async-done | bytes 131088 | tf_op jit(solution)/shard_map/reduce_scatter | solution.py:40
  1109.8 0.0 copy-done.1
  1109.8 0.0 copy-done.2
  1109.8 0.0 copy-done.3
  1109.8 0.9 multiply_convert_fusion.1
  1110.7 0.0 copy-start
  1110.7 3.9 gather_fusion
  1114.7 0.0 copy-done
  1114.7 1.1 select_select_fusion
  1115.8 0.0 all-reduce.2.cloned.1.call-update
  1115.9 264.5 %all-reduce.2.cloned.1.call-done = bf16[1024,256]{1,0:T(8,128)(2,1)} async-done(((bf16[1024,256]{1,0:T(8,128)(2,1)}), bf16[1024,256]{1,0:T(8,128)(2,1)}) %all-reduce.2.cloned.1.call-update) | async-done | bytes 524304 | tf_op jit(solution)/shard_map/psum | solution.py:23
  1380.4 0.0 copy-done.6
  1380.4 2.0 fusion.8
  (7 shorter events, 0.0 us)
Async XLA Ops:
  7.2 133.3 %all-gather.4.cloned.1.call-start = ((), (), s32[]{:S(2)}) async-start(), calls=%async_computation.7 | async-start | bytes 2162688 | tf_op jit(solution)/shard_map/all_gather | solution.py:41
  7.9 188.7 %reduce-scatter.9.cloned.1.call-start = ((), (), s32[]{:S(2)}) async-start(), calls=%async_computation.8 | async-start | bytes 294912 | tf_op jit(solution)/shard_map/reduce_scatter | solution.py:43
  140.5 3.2 copy-start.5
  143.6 276.2 %reduce-scatter.7.cloned.1.call-start = ((), (), s32[]{:S(2)}) async-start(), calls=%async_computation.6 | async-start | bytes 4325376 | tf_op jit(solution)/shard_map/reduce_scatter | solution.py:40
  188.7 456.4 %reduce-scatter.11.cloned.1.call-start = ((), (), s32[]{:S(2)}) async-start(), calls=%async_computation.9 | async-start | bytes 4325376 | tf_op jit(solution)/shard_map/reduce_scatter | solution.py:40
  215.4 509.0 %all-gather.6.cloned.1.call-start = ((), (), s32[]{:S(2)}) async-start(), calls=%async_computation.10 | async-start | bytes 2162688 | tf_op jit(solution)/shard_map/all_gather | solution.py:41
  421.3 381.2 %all-gather.8.cloned.1.call-start = ((), (), s32[]{:S(2)}) async-start(), calls=%async_computation.13 | async-start | bytes 2162688 | tf_op jit(solution)/shard_map/all_gather | solution.py:41
  646.6 191.7 %reduce-scatter.13.cloned.1.call-start = ((), (), s32[]{:S(2)}) async-start(), calls=%async_computation.11 | async-start | bytes 294912 | tf_op jit(solution)/shard_map/reduce_scatter | solution.py:43
  727.5 145.6 %copy-start.4 = (f32[32,256]{1,0:T(8,128)S(1)}, f32[32,256]{1,0:T(8,128)}, u32[]{:S(2)}) copy-start(f32[32,256]{1,0:T(8,128)} %reduce-scatter.9.cloned.1.call-done) | copy-start | bytes 98308
  727.5 145.6 %reduce-scatter.17.cloned.1.call-start = ((), (), s32[]{:S(2)}) async-start(), calls=%async_computation.14 | async-start | bytes 294912 | tf_op jit(solution)/shard_map/reduce_scatter | solution.py:43
  805.6 304.2 %reduce-scatter.15.cloned.1.call-start = ((), (), s32[]{:S(2)}) async-start(), calls=%async_computation.12 | async-start | bytes 4325376 | tf_op jit(solution)/shard_map/reduce_scatter | solution.py:40
  873.9 506.5 %copy-start.6 = (bf16[32,256]{1,0:T(8,128)(2,1)}, bf16[32,256]{1,0:T(8,128)(2,1)S(1)}, u32[]{:S(2)}) copy-start(bf16[32,256]{1,0:T(8,128)(2,1)S(1)} %get-tuple-element.5) | copy-start | bytes 49156
  891.9 0.7 copy-start.7
  891.9 217.9 %copy-start.1 = (f32[128,256]{1,0:T(8,128)S(1)}, f32[128,256]{1,0:T(8,128)}, u32[]{:S(2)}) copy-start(f32[128,256]{1,0:T(8,128)} %reduce-scatter.7.cloned.1.call-done) | copy-start | bytes 393220
  891.9 217.9 %copy-start.2 = (f32[128,256]{1,0:T(8,128)S(1)}, f32[128,256]{1,0:T(8,128)}, u32[]{:S(2)}) copy-start(f32[128,256]{1,0:T(8,128)} %reduce-scatter.11.cloned.1.call-done) | copy-start | bytes 393220
  891.9 217.9 %copy-start.3 = (bf16[128,256]{1,0:T(8,128)(2,1)S(1)}, bf16[128,256]{1,0:T(8,128)(2,1)}, u32[]{:S(2)}) copy-start(bf16[128,256]{1,0:T(8,128)(2,1)} %param.5) | copy-start | bytes 196612
  891.9 488.4 %all-reduce.2.cloned.1.call-start = ((), (), s32[]{:S(2)}) async-start(), calls=%async_computation.15 | async-start | bytes 1048576 | tf_op jit(solution)/shard_map/psum | solution.py:23
  1110.7 4.0 copy-start
Sparse Core Ops, SparseCore 0:
  10.6 77.0 all-gather.3
  143.7 52.8 reduce-scatter.8
  200.5 219.2 reduce-scatter.6
  423.5 221.4 reduce-scatter.10
  648.1 76.3 all-gather.5
  727.5 75.0 all-gather.7
  805.0 33.2 reduce-scatter.12
  840.8 32.2 reduce-scatter.16
  892.1 217.6 reduce-scatter.14
  1116.0 264.3 all-reduce.1
where the time goes:
time: 1390 us
  waiting for transfers between devices  1140 us (82%)
  blocking collectives  200 us (14%)
  matrix products  19 us (1%)
  between operations  14.3 us (1%)
    reduce_scatter x3, waiting for transfers between devices, device_step(): lax.psum_scatter(user_part, 'col', scatter_dimension=0, tiled=True)  645 us
    psum x1, waiting for transfers between devices, query_scores(): picked = lax.psum(picked, ('row', 'col'))  265 us
    all_gather x3, waiting for transfers between devices, device_step(): user_panel = lax.all_gather(user_cur, 'col', axis=0, tiled=True)  153 us
    psum x1, blocking collectives, norm_block(): deg_user = lax.psum(jnp.sum(mask_blk, axis=1), 'col')  119 us
    reduce_scatter x3, waiting for transfers between devices, device_step(): lax.psum_scatter(item_part, 'row', scatter_dimension=0, tiled=True)  75.3 us
    all_gather x3, blocking collectives, device_step(): item_panel = lax.all_gather(item_cur, 'row', axis=0, tiled=True)  73.2 us
  transfers between devices with their start and end apart: 10, of which 9 were waited for; matrix products, arithmetic and copies ran while one was open for 1% of the time, Pallas kernels for 0%

commit v1 on v0

v1 whole, which is shorter than its diff:
```python
import jax
import jax.numpy as jnp
from jax import lax
from jax.experimental import pallas as pl
from jax.experimental.pallas import tpu as pltpu
from jax.sharding import PartitionSpec as P

LAYERS = 3
Z, Y, R = 8, 4, 8
G = Y * R
UB, IB = 128, 32
E = 256
NQ = 1024
QB = NQ // G
H = UB // 2
F32, BF16 = jnp.float32, jnp.bfloat16
MESH = pl.DeviceIdType.MESH
CONTRACT_ROWS = (((0,), (0,)), ((), ()))
CONTRACT_LANES = (((1,), (1,)), ((), ()))


def remote(src, dst, send_sem, recv_sem, col, row):
    return pltpu.make_async_remote_copy(src_ref=src, dst_ref=dst, send_sem=send_sem, recv_sem=recv_sem,
                                        device_id=(col, row), device_id_type=MESH)


def wait_bytes(ref, sem):
    pltpu.make_async_copy(ref, ref, sem).wait()


def kernel(mask_ref, user_ref, item_ref, query_ref, fu_ref, fi_ref, sc_ref,
           mask_v, msend, mrecv, adj, rs_send, rs_recv, cs_send, cs_recv, invu, invi,
           eu_pan, ei_pan, up, us, ur, ip, ir, qs, qr, qz, qzs, qall, usum, isum,
           load_sem, mask_ssem, mask_rsem, rs_ssem, rs_rsem, cs_ssem, cs_rsem,
           eu0_ssem, eu0_rsem, ei_ssem, ei_rsem, us_ssem, us_rsem, ip_ssem, ip_rsem,
           ag_ssem, ag_rsem, q_ssem, q_rsem):
    col = lax.axis_index('col')
    row = lax.axis_index('row')
    z, y = lax.div(col, Y), lax.rem(col, Y)
    me = y * R + row

    def zat(d):
        return lax.rem(z + (d % Z), Z)

    def plane():
        for slot in range(1, G):
            py = lax.rem(y + slot // R, Y)
            pr = lax.rem(row + slot % R, R)
            yield slot - 1, py, pr, py * R + pr

    order = [4, 3, -3, 2, -2, 1, -1, 0]

    barrier = pltpu.get_barrier_semaphore()
    for d in range(1, Z * Y):
        pl.semaphore_signal(barrier, inc=1, device_id=(lax.rem(col + d, Z * Y), row), device_id_type=MESH)
    for slot, py, pr, g in plane():
        if (slot + 1) % R:
            pl.semaphore_signal(barrier, inc=1, device_id=(z * Y + py, pr), device_id_type=MESH)

    loads = []
    for j, d in enumerate(order):
        zc = zat(d)
        load = pltpu.make_async_copy(mask_ref.at[pl.ds(zc * (Y * UB), Y * UB)], mask_v.at[j], load_sem.at[j])
        load.start()
        loads.append(load)
    ones_w = jnp.ones((8, E), BF16)
    ones_h = jnp.ones((8, UB), BF16)
    cs_send[...] = jnp.zeros_like(cs_send)
    for j, d in enumerate(order):
        zc = zat(d)
        loads[j].wait()
        for p in range(Y):
            block = mask_v[j, p * UB:(p + 1) * UB, :].astype(F32).astype(BF16)
            msend[p, j] = block
            sums = lax.dot_general(ones_w, block, CONTRACT_LANES, preferred_element_type=F32)
            rs_send[p, pl.ds(zc, 1), :] = sums[0:1]
            cs_send[...] += jnp.dot(ones_h, block, preferred_element_type=F32)
    cs_recv[me] = cs_send[...]
    eu_pan[0, z] = user_ref[...]
    ei_pan[0, me] = item_ref[...]

    pl.semaphore_wait(barrier, 31 + 28)

    for d in range(1, Z * Y):
        pc = lax.rem(col + d, Z * Y)
        remote(rs_send.at[lax.rem(pc, Y)], rs_recv.at[d - 1], rs_ssem, rs_rsem, pc, row).start()
    for slot, py, pr, g in plane():
        remote(cs_send, cs_recv.at[me], cs_ssem, cs_rsem, z * Y + py, pr).start()
    for slot, py, pr, g in plane():
        remote(item_ref, ei_pan.at[0, me], ei_ssem.at[0], ei_rsem.at[0], z * Y + py, pr).start()
    for d in range(1, Z):
        remote(user_ref, eu_pan.at[0, z], eu0_ssem, eu0_rsem, zat(d) * Y + y, row).start()
    for j in range(Z):
        for d in range(1, Y):
            py = lax.rem(y + d, Y)
            remote(msend.at[py, j], mrecv.at[j, d - 1], mask_ssem, mask_rsem.at[j], z * Y + py, row).start()

    wait_bytes(rs_recv, rs_rsem)
    deg = rs_send[y]
    for d in range(Z * Y - 1):
        deg = deg + rs_recv[d]
    invu[...] = lax.rsqrt(jnp.maximum(deg, 1.0))
    wait_bytes(cs_recv.at[pl.ds(0, G - 1)], cs_rsem)
    for s in range(Y):
        deg = cs_recv[s * R]
        for r in range(1, R):
            deg = deg + cs_recv[s * R + r]
        invi[s] = lax.rsqrt(jnp.maximum(deg, 1.0))

    def make_adj(j, zc):
        wait_bytes(mrecv.at[j], mask_rsem.at[j])
        iu = jnp.broadcast_to(invu[pl.ds(zc, 1), :], (UB, UB)).T
        iu = jnp.concatenate([iu, iu], axis=1)
        for d in range(Y):
            s = lax.rem(y + (Y - d), Y)
            m = (msend[y, j] if d == 0 else mrecv[j, d - 1]).astype(F32)
            adj[s, zc] = ((iu * m) * invi[s][0:1, :]).astype(BF16)

    def user_piece(k, j):
        zc = zat(order[j])
        if k == 0:
            make_adj(j, zc)
        acc = None
        for s in range(Y):
            t = jnp.dot(adj[s, zc], ei_pan[k, s * R:(s + 1) * R].reshape(R * IB, E), preferred_element_type=F32)
            acc = t if acc is None else acc + t
        up[j] = acc

    piece_of = {d: j for j, d in enumerate(order)}
    right, left = zat(1) * Y + y, zat(-1) * Y + y

    def item_parts(k):
        eu = eu_pan[k].reshape(Z * UB, E)
        for s in range(Y):
            part = lax.dot_general(adj[s].reshape(Z * UB, E), eu, CONTRACT_ROWS, preferred_element_type=F32)
            ip[k, s * R:(s + 1) * R] = part.reshape(R, IB, E)
        for slot, py, pr, g in plane():
            remote(ip.at[k, g], ir.at[k, slot], ip_ssem.at[k], ip_rsem.at[k], z * Y + py, pr).start()

    def item_total(k):
        wait_bytes(ir.at[k], ip_rsem.at[k])
        total = ip[k, me]
        for slot in range(G - 1):
            total = total + ir[k, slot]
        return total

    def user_total(k, before_last):
        def send(way, step, c):
            rows = pl.ds(c * H, H)
            remote(us.at[k, way, step, rows], ur.at[k, way, step, rows], us_ssem.at[k], us_rsem.at[k, way, step, c],
                   right if way == 0 else left, row).start()

        def got(way, step, c):
            rows = pl.ds(c * H, H)
            wait_bytes(ur.at[k, way, step, rows], us_rsem.at[k, way, step, c])
            return ur[k, way, step, c * H:(c + 1) * H]

        def own(way, step, c):
            j = piece_of[4 - step] if way == 0 or step == 0 else piece_of[step - 4]
            return up[j, c * H:(c + 1) * H]

        def emit(way, step, c, first):
            value = own(way, step, c)
            if not first:
                value = value + got(way, step - 1, c)
            us[k, way, step, c * H:(c + 1) * H] = value
            send(way, step, c)

        user_piece(k, 0)
        emit(0, 0, 0, True)
        emit(1, 0, 1, True)
        user_piece(k, 1)
        emit(0, 1, 1, True)
        user_piece(k, 2)
        emit(1, 1, 0, True)
        for step in range(1, 4):
            emit(0, step, 0, False)
            emit(1, step, 1, False)
            if step < 3:
                user_piece(k, 2 * step + 1)
                user_piece(k, 2 * step + 2)
                emit(0, step + 1, 1, False)
                emit(1, step + 1, 0, False)
        user_piece(k, 7)
        before_last()
        halves = []
        for c in range(2):
            halves.append(up[7, c * H:(c + 1) * H] + got(0, 3, c) + got(1, 3, c))
        return jnp.concatenate(halves, axis=0)

    def gather_user(k):
        def send(way, step, c):
            src = eu_pan.at[k, zat(-step if way == 0 else step), pl.ds(c * H, H)]
            remote(src, src, ag_ssem.at[k], ag_rsem.at[k, way, step, c], right if way == 0 else left, row).start()

        def got(way, step, c):
            dst = eu_pan.at[k, zat(-step - 1 if way == 0 else step + 1), pl.ds(c * H, H)]
            wait_bytes(dst, ag_rsem.at[k, way, step, c])

        def begin():
            for c in range(2):
                send(0, 0, c)
                send(1, 0, 1 - c)

        def rest():
            for step in range(3):
                for c in range(2):
                    for way in range(2):
                        cc = c if way == 0 else 1 - c
                        got(way, step, cc)
                        if step < 2 or c == 0:
                            send(way, step + 1, cc)
            got(0, 3, 0)
            got(1, 3, 1)

        return begin, rest

    usum[...] = user_ref[...].astype(F32)
    isum[...] = item_ref[...].astype(F32)
    wait_bytes(ei_pan.at[0, pl.ds(0, G - 1)], ei_rsem.at[0])

    for k in range(LAYERS):
        if k == 0:
            def start_items():
                wait_bytes(eu_pan.at[0, pl.ds(0, Z - 1)], eu0_rsem)
                item_parts(0)
            new_user = user_total(k, start_items).astype(BF16)
        else:
            item_parts(k)
            wait_bytes(ei_pan.at[k, pl.ds(0, G - 1)], ei_rsem.at[k])
            new_user = user_total(k, lambda: None).astype(BF16)
        usum[...] += new_user.astype(F32)
        if k + 1 < LAYERS:
            eu_pan[k + 1, z] = new_user
            begin, rest = gather_user(k + 1)
            begin()
            new_item = item_total(k).astype(BF16)
            isum[...] += new_item.astype(F32)
            ei_pan[k + 1, me] = new_item
            for slot, py, pr, g in plane():
                own = ei_pan.at[k + 1, me]
                remote(own, own, ei_ssem.at[k + 1], ei_rsem.at[k + 1], z * Y + py, pr).start()
            rest()

    final_user = (usum[...] / (LAYERS + 1)).astype(BF16)
    fu_ref[...] = final_user

    base = (row * (Z * Y) + col) * UB
    ids = lax.broadcasted_iota(jnp.int32, (UB, NQ), 0) + base
    hot = jnp.where(ids == query_ref[...], 1.0, 0.0).astype(BF16)
    qs[...] = lax.dot_general(hot, final_user, CONTRACT_ROWS, preferred_element_type=F32).astype(BF16).reshape(G, QB, E)
    for slot, py, pr, g in plane():
        remote(qs.at[g], qr.at[slot], q_ssem.at[0], q_rsem.at[0], z * Y + py, pr).start()

    new_item = item_total(LAYERS - 1).astype(BF16)
    final_item = ((isum[...] + new_item.astype(F32)) / (LAYERS + 1)).astype(BF16)
    fi_ref[...] = final_item

    wait_bytes(qr, q_rsem.at[0])
    total = qs[me].astype(F32)
    for slot in range(G - 1):
        total = total + qr[slot].astype(F32)
    qzs[...] = total.astype(BF16)
    for d in range(1, Z):
        remote(qzs, qz.at[d - 1], q_ssem.at[1], q_rsem.at[1], zat(d) * Y + y, row).start()
    wait_bytes(qz, q_rsem.at[1])
    for d in range(Z - 1):
        total = total + qz[d].astype(F32)
    qall[me] = total.astype(BF16)
    for slot, py, pr, g in plane():
        remote(qall.at[me], qall.at[me], q_ssem.at[2], q_rsem.at[2], z * Y + py, pr).start()
    wait_bytes(qall.at[pl.ds(0, G - 1)], q_rsem.at[2])
    sc_ref[...] = lax.dot_general(qall[...].reshape(NQ, E), final_item, CONTRACT_LANES, preferred_element_type=F32)

    wait_bytes(rs_recv, rs_ssem)
    wait_bytes(cs_recv.at[pl.ds(0, G - 1)], cs_ssem)
    wait_bytes(eu_pan.at[0, pl.ds(0, Z - 1)], eu0_ssem)
    wait_bytes(msend.at[pl.ds(0, Y - 1)], mask_ssem)
    for k in range(LAYERS):
        wait_bytes(ei_pan.at[k, pl.ds(0, G - 1)], ei_ssem.at[k])
        wait_bytes(ir.at[k], ip_ssem.at[k])
        wait_bytes(up.at[pl.ds(0, 7)], us_ssem.at[k])
        if k:
            wait_bytes(eu_pan.at[k, pl.ds(0, 7)], ag_ssem.at[k])
    wait_bytes(qr, q_ssem.at[0])
    wait_bytes(qz, q_ssem.at[1])
    wait_bytes(qall.at[pl.ds(0, G - 1)], q_ssem.at[2])


def propagate(mask, user, item, queries):
    dma = pltpu.SemaphoreType.DMA
    vmem = pl.BlockSpec(memory_space=pltpu.VMEM)
    L = LAYERS
    return pl.pallas_call(
        kernel,
        out_shape=(jax.ShapeDtypeStruct((UB, E), BF16), jax.ShapeDtypeStruct((IB, E), BF16),
                   jax.ShapeDtypeStruct((NQ, IB), F32)),
        in_specs=[pl.BlockSpec(memory_space=pl.ANY), vmem, vmem, vmem],
        out_specs=(vmem, vmem, vmem),
        scratch_shapes=[
            pltpu.VMEM((Z, Y * UB, E), jnp.int32),
            pltpu.VMEM((Y, Z, UB, E), BF16),
            pltpu.VMEM((Z, Y - 1, UB, E), BF16),
            pltpu.VMEM((Y, Z, UB, E), BF16),
            pltpu.VMEM((Y, Z, UB), F32),
            pltpu.VMEM((Z * Y - 1, Z, UB), F32),
            pltpu.VMEM((8, E), F32),
            pltpu.VMEM((G, 8, E), F32),
            pltpu.VMEM((Z, UB), F32),
            pltpu.VMEM((Y, 8, E), F32),
            pltpu.VMEM((L, Z, UB, E), BF16),
            pltpu.VMEM((L, G, IB, E), BF16),
            pltpu.VMEM((Z, UB, E), F32),
            pltpu.VMEM((L, 2, 4, UB, E), F32),
            pltpu.VMEM((L, 2, 4, UB, E), F32),
            pltpu.VMEM((L, G, IB, E), F32),
            pltpu.VMEM((L, G - 1, IB, E), F32),
            pltpu.VMEM((G, QB, E), BF16),
            pltpu.VMEM((G - 1, QB, E), BF16),
            pltpu.VMEM((Z - 1, QB, E), BF16),
            pltpu.VMEM((QB, E), BF16),
            pltpu.VMEM((G, QB, E), BF16),
            pltpu.VMEM((UB, E), F32),
            pltpu.VMEM((IB, E), F32),
            dma((Z,)), dma, dma((Z,)), dma, dma, dma, dma,
            dma, dma, dma((L,)), dma((L,)), dma((L,)), dma((L, 2, 4, 2)), dma((L,)), dma((L,)),
            dma((L,)), dma((L, 2, 4, 2)), dma((3,)), dma((3,)),
        ],
        compiler_params=pltpu.CompilerParams(collective_id=0, has_side_effects=True, vmem_limit_bytes=60 * 2**20),
    )(mask, user, item, queries.reshape(1, NQ))


def solution(mesh):
    return jax.shard_map(propagate, mesh=mesh,
                         in_specs=(P('row', 'col'), P(('row', 'col'), None), P(('col', 'row'), None), P()),
                         out_specs=(P(('row', 'col'), None), P(('col', 'row'), None), P(None, ('col', 'row'))),
                         check_vma=False)
```

time: 1390 us -> 149 us (0.11)
  waiting for transfers between devices: 1140 us -> 0 us
  blocking collectives: 200 us -> 0 us
  Pallas kernels: 0 us -> 144 us
  matrix products: 19 us -> 0 us
    reduce_scatter x6 -> x0, waiting for transfers between devices: 720 us -> none  [the longest x3 645 us: device_step(): lax.psum_scatter(user_part, 'col', scatter_dimension=0, tiled=True)]
    psum x1 -> x0, waiting for transfers between devices: 265 us -> none  [query_scores(): picked = lax.psum(picked, ('row', 'col'))]
    all_gather x3 -> x0, waiting for transfers between devices: 153 us -> none  [device_step(): user_panel = lax.all_gather(user_cur, 'col', axis=0, tiled=True)]
    pallas_call x0 -> x1, Pallas kernels: none -> 144 us  [propagate(): pl.pallas_call(kernel, out_shape=(jax.ShapeDtypeStruct((UB, E), BF16), ja...]
    psum x2 -> x0, blocking collectives: 127 us -> none  [the longest x1 119 us: norm_block(): deg_user = lax.psum(jnp.sum(mask_blk, axis=1), 'col')]
    all_gather x3 -> x0, blocking collectives: 73.2 us -> none  [device_step(): item_panel = lax.all_gather(item_cur, 'row', axis=0, tiled=True)]
    dot_general x7 -> x0, matrix products: 19 us -> none  [the longest x3 9.11 us: device_step(): lax.dot_general(norm_adj, user_panel, contract_rows, preferred_element_ty...]
  transfers between devices with their start and end apart: 10 -> 0, of which waited for: 9 -> 0; matrix products, arithmetic and copies ran while one was open for 1% -> 0% of each run, Pallas kernels for 0% -> 0%
where the time goes in v1:
time: 149 us
  Pallas kernels  144 us (97%)
  local copies, waits for them, and re-layouts  4.67 us (3%)
    pallas_call x1, Pallas kernels, propagate(): pl.pallas_call(kernel, out_shape=(jax.ShapeDtypeStruct((UB, E), BF16), ja...  144 us

profile of v1, /device:TPU:1, one launch (start us, length us, event | category | flops | bytes accessed | tf_op | source)
XLA Modules:
  0.0 149.0 jit_solution(17286381074898109508)
XLA Ops:
  0.6 143.7 %shard_map.67 = (bf16[128,256]{1,0:T(8,128)(2,1)}, bf16[32,256]{1,0:T(8,128)(2,1)}, f32[1024,32]{1,0:T(8,128)}) custom-call(s32[4096,256]{1,0:T(8,128)} %mask_ref.1, bf16[128,256]{1,0:T(8,128)(2,1)} %user_ref.1, bf16[32,256]{1,0:T(8,128)(2,1)} %item_ref.1, s32[1,1024]{1,0:T(1,128)} %bitcast.1), custom_call_target="tpu_custom_call" | custom-call | tf_op jit(solution)/shard_map/pallas_call | solution.py:294
  144.3 1.9 %copy.7 = f32[1024,32]{0,1:T(8,128)} copy(f32[1024,32]{1,0:T(8,128)} %get-tuple-element.5) | data formatting | bytes 262144 | tf_op jit(solution)/shard_map/pallas_call | solution.py:294
  146.2 1.5 copy.10
  147.6 1.3 copy.11

commit v2 on v1

v2 whole, which is shorter than its diff:
```python
import jax
import jax.numpy as jnp
from jax import lax
from jax.experimental import pallas as pl
from jax.experimental.pallas import tpu as pltpu
from jax.sharding import PartitionSpec as P

LAYERS = 3
Z, Y, X = 8, 4, 4
R = 2 * X
G = Y * R
UB, IB = 128, 32
E = 256
NQ = 1024
QB = NQ // G
H = UB // 2
F32, BF16 = jnp.float32, jnp.bfloat16
MESH = pl.DeviceIdType.MESH
CONTRACT_ROWS = (((0,), (0,)), ((), ()))
CONTRACT_LANES = (((1,), (1,)), ((), ()))


def remote(src, dst, send_sem, recv_sem, col, row):
    return pltpu.make_async_remote_copy(src_ref=src, dst_ref=dst, send_sem=send_sem, recv_sem=recv_sem,
                                        device_id=(col, row), device_id_type=MESH)


def wait_bytes(ref, sem):
    pltpu.make_async_copy(ref, ref, sem).wait()


def kernel(mask_ref, user_ref, item_ref, query_ref, fu_ref, fi_ref, sc_ref,
           mask_v, msend, mrecv, adj, adjt, rs_send, rs_recv, cs_send, cs_recv, invu, invi,
           eu_pan, ei_pan, up, us, ur, ip, pr, iq, ir, hot, qs, qp, qt, qr, qz, qzs, qall, usum, isum,
           load_sem, mask_ssem, mask_rsem, rs_ssem, rs_rsem, cs_ssem, cs_rsem,
           eu0_ssem, eu0_rsem, ei_ssem, ei_rsem, fw_ssem, fw_rsem, us_ssem, us_rsem,
           pr_ssem, pr_rsem, ip_ssem, ip_rsem, ag_ssem, ag_rsem, q_ssem, q_rsem, qg_rsem, qf_rsem):
    col = lax.axis_index('col')
    row = lax.axis_index('row')
    z, y = lax.div(col, Y), lax.rem(col, Y)
    x, c = lax.div(row, 2), lax.rem(row, 2)
    other = 1 - c
    partner = x * 2 + other
    me = y * R + row
    spot = y * X + x

    def zat(d):
        return lax.rem(z + (d % Z), Z)

    def yat(d):
        return lax.rem(y + (d % Y), Y)

    def plane():
        for dy in (2, 1, 3, 0):
            for dx in (2, 1, 3, 0):
                if dy or dx:
                    yield dy * X + dx - 1, dy, yat(dy), lax.rem(x + dx, X)

    order = [4, 3, -3, 2, -2, 1, -1, 0]
    piece_of = {d: j for j, d in enumerate(order)}
    right, left = zat(1) * Y + y, zat(-1) * Y + y

    loads = []
    for j, d in enumerate(order):
        zc = zat(d)
        load = pltpu.make_async_copy(mask_ref.at[pl.ds(zc * (Y * UB), Y * UB)], mask_v.at[j], load_sem.at[j])
        load.start()
        loads.append(load)

    barrier = pltpu.get_barrier_semaphore()
    for d in range(1, Z * Y):
        pl.semaphore_signal(barrier, inc=1, device_id=(lax.rem(col + d, Z * Y), row), device_id_type=MESH)
    for dy in range(Y):
        for dr in range(1, R):
            pl.semaphore_signal(barrier, inc=1, device_id=(z * Y + yat(dy), lax.rem(row + dr, R)), device_id_type=MESH)

    ones_w = jnp.ones((8, E), BF16)
    colsum = jnp.zeros((8, E), F32)
    for j, d in enumerate(order):
        zc = zat(d)
        loads[j].wait()
        for p in range(Y):
            wide = mask_v[j, p * UB:(p + 1) * UB, :].astype(F32)
            block = wide.astype(BF16)
            msend[p, j] = block
            sums = lax.dot_general(ones_w, block, CONTRACT_LANES, preferred_element_type=F32)
            rs_send[p, pl.ds(zc, 1), :] = sums[0:1]
            colsum = colsum + jnp.sum(wide.reshape(UB // 8, 8, E), axis=0)
    cs_send[...] = jnp.sum(colsum, axis=0, keepdims=True)
    cs_recv[me] = cs_send[...]
    eu_pan[0, z] = user_ref[...]
    ei_pan[0, c, spot] = item_ref[...]

    pl.semaphore_wait(barrier, 31 + 28)

    for dy in range(Y):
        for dr in range(R):
            if dy or dr:
                remote(cs_send, cs_recv.at[me], cs_ssem, cs_rsem, z * Y + yat(dy), lax.rem(row + dr, R)).start()
    for d in range(1, Z * Y):
        pc = lax.rem(col + d, Z * Y)
        remote(rs_send.at[lax.rem(pc, Y)], rs_recv.at[d - 1], rs_ssem, rs_rsem, pc, row).start()
    for slot, dy, py, px in plane():
        remote(item_ref, ei_pan.at[0, c, spot], ei_ssem.at[0], ei_rsem.at[0, dy], z * Y + py, px * 2 + c).start()
    for d in range(1, Z):
        remote(user_ref, eu_pan.at[0, z], eu0_ssem, eu0_rsem, zat(d) * Y + y, row).start()
    for j in range(Z):
        for d in range(1, Y):
            py = yat(d)
            remote(msend.at[py, j], mrecv.at[j, d - 1], mask_ssem, mask_rsem.at[j], z * Y + py, row).start()

    usum[...] = user_ref[...].astype(F32)
    isum[...] = item_ref[...].astype(F32)
    base = (row * (Z * Y) + col) * UB
    ids = lax.broadcasted_iota(jnp.int32, (UB, NQ), 0) + base
    hot[...] = jnp.where(ids == query_ref[...], 1.0, 0.0).T.astype(BF16)

    wait_bytes(cs_recv.at[pl.ds(0, G - 1)], cs_rsem)
    for s in range(Y):
        deg = cs_recv[s * R]
        for r in range(1, R):
            deg = deg + cs_recv[s * R + r]
        invi[s] = lax.rsqrt(jnp.maximum(deg, 1.0))
    wait_bytes(rs_recv, rs_rsem)
    deg = rs_send[y]
    for d in range(Z * Y - 1):
        deg = deg + rs_recv[d]
    invu[...] = lax.rsqrt(jnp.maximum(deg, 1.0))

    def make_adj(j, zc):
        wait_bytes(mrecv.at[j], mask_rsem.at[j])
        iu = jnp.broadcast_to(invu[pl.ds(zc, 1), :], (UB, UB)).T
        iu = jnp.concatenate([iu, iu], axis=1)
        for d in range(Y):
            s = yat(-d)
            m = (msend[y, j] if d == 0 else mrecv[j, d - 1]).astype(F32)
            a = (iu * m) * invi[s]
            adj[s, zc] = a.astype(BF16)
            adjt[s, :, pl.ds(pl.multiple_of(zc * UB, UB), UB)] = a.T.astype(BF16)

    def user_piece(k, j):
        zc = zat(order[j])
        if k == 0:
            make_adj(j, zc)
        acc = None
        for s in range(Y):
            panel = jnp.concatenate([ei_pan[k, cc, s * X + xx] for xx in range(X) for cc in range(2)], axis=0)
            t = jnp.dot(adj[s, zc], panel, preferred_element_type=F32)
            acc = t if acc is None else acc + t
        up[j] = acc

    def item_parts(k):
        eu = eu_pan[k].reshape(Z * UB, E)
        for j, dy in enumerate((2, 1, 3, 0)):
            s = yat(dy)
            part = jnp.dot(adjt[s], eu, preferred_element_type=F32).reshape(X, 2, IB, E)
            for xx in range(X):
                for cc in range(2):
                    ip[k, cc, s * X + xx] = part[xx, cc]
            remote(ip.at[k, other, pl.ds(s * X, X)], pr.at[k, j], pr_ssem.at[k], pr_rsem.at[k, j], col, partner).start()
        for j, dy in enumerate((2, 1, 3, 0)):
            s = yat(dy)
            wait_bytes(pr.at[k, j], pr_rsem.at[k, j])
            iq[k, pl.ds(s * X, X)] = ip[k, c, pl.ds(s * X, X)] + pr[k, j]
            for slot, dy2, py, px in plane():
                if dy2 == dy:
                    remote(iq.at[k, s * X + px], ir.at[k, slot], ip_ssem.at[k], ip_rsem.at[k], z * Y + py, px * 2 + c).start()

    def item_total(k):
        wait_bytes(ir.at[k], ip_rsem.at[k])
        total = iq[k, spot]
        for slot in range(G // 2 - 1):
            total = total + ir[k, slot]
        return total

    def gather_plane(pan, ssem, rsem):
        for slot, dy, py, px in plane():
            remote(pan.at[c, spot], pan.at[c, spot], ssem, rsem.at[dy], z * Y + py, px * 2 + c).start()

    def forward_plane(pan, rsem, fssem, frsem):
        for dy in (0, 1, 3, 2):
            n = X - 1 if dy == 0 else X
            rows = pl.ds(yat(-dy) * X, X)
            wait_bytes(pan.at[c, pl.ds(0, n)], rsem.at[dy])
            remote(pan.at[c, rows], pan.at[c, rows], fssem, frsem.at[dy], col, partner).start()

    def wait_plane(pan, frsem):
        for dy in (0, 1, 3, 2):
            wait_bytes(pan.at[other, pl.ds(yat(-dy) * X, X)], frsem.at[dy])

    def user_total(k, hooks):
        def send(way, step, h):
            rows = pl.ds(h * H, H)
            remote(us.at[k, way, step, rows], ur.at[k, way, step, rows], us_ssem.at[k], us_rsem.at[k, way, step, h],
                   right if way == 0 else left, row).start()

        def got(way, step, h):
            rows = pl.ds(h * H, H)
            wait_bytes(ur.at[k, way, step, rows], us_rsem.at[k, way, step, h])
            return ur[k, way, step, h * H:(h + 1) * H]

        def emit(way, step, h, first):
            j = piece_of[4 - step] if way == 0 or step == 0 else piece_of[step - 4]
            value = up[j, h * H:(h + 1) * H]
            if not first:
                value = value + got(way, step - 1, h)
            us[k, way, step, h * H:(h + 1) * H] = value
            send(way, step, h)

        user_piece(k, 0)
        emit(0, 0, 0, True)
        emit(1, 0, 1, True)
        user_piece(k, 1)
        emit(0, 1, 1, True)
        user_piece(k, 2)
        emit(1, 1, 0, True)
        for step in range(1, 4):
            if step < 3:
                user_piece(k, 2 * step + 1)
                user_piece(k, 2 * step + 2)
            else:
                user_piece(k, 7)
            emit(0, step, 0, False)
            emit(1, step, 1, False)
            if step < 3:
                emit(0, step + 1, 1, False)
                emit(1, step + 1, 0, False)
            if step in hooks:
                hooks[step]()
        halves = []
        for h in range(2):
            halves.append(up[7, h * H:(h + 1) * H] + got(0, 3, h) + got(1, 3, h))
        new_user = jnp.concatenate(halves, axis=0).astype(BF16)
        usum[...] += new_user.astype(F32)
        return new_user

    def gather_user(k):
        def send(way, step, h):
            src = eu_pan.at[k, zat(-step if way == 0 else step), pl.ds(h * H, H)]
            remote(src, src, ag_ssem.at[k], ag_rsem.at[k, way, step, h], right if way == 0 else left, row).start()

        def got(way, step, h):
            dst = eu_pan.at[k, zat(-step - 1 if way == 0 else step + 1), pl.ds(h * H, H)]
            wait_bytes(dst, ag_rsem.at[k, way, step, h])

        def begin(new_user):
            eu_pan[k, z] = new_user
            for h in range(2):
                send(0, 0, h)
                send(1, 0, 1 - h)

        def hop(step):
            for h in range(2):
                for way in range(2):
                    hh = h if way == 0 else 1 - h
                    got(way, step, hh)
                    if step < 2 or h == 0:
                        send(way, step + 1, hh)

        def last():
            got(0, 3, 0)
            got(1, 3, 1)

        return begin, hop, last

    def items_next(k):
        new_item = item_total(k).astype(BF16)
        isum[...] += new_item.astype(F32)
        ei_pan[k + 1, c, spot] = new_item
        gather_plane(ei_pan.at[k + 1], ei_ssem.at[k + 1], ei_rsem.at[k + 1])

    def items_forward(k):
        forward_plane(ei_pan.at[k], ei_rsem.at[k], fw_ssem.at[k], fw_rsem.at[k])

    def items_wait(k):
        wait_plane(ei_pan.at[k], fw_rsem.at[k])

    items_forward(0)
    items_wait(0)
    new_user = user_total(0, {})
    begin1, hop1, last1 = gather_user(1)
    begin1(new_user)
    wait_bytes(eu_pan.at[0, pl.ds(0, Z - 1)], eu0_rsem)
    item_parts(0)
    for step in range(3):
        hop1(step)
    last1()
    item_parts(1)
    items_next(0)
    items_forward(1)
    items_wait(1)
    new_user = user_total(1, {2: lambda: items_next(1), 3: lambda: items_forward(2)})
    begin2, hop2, last2 = gather_user(2)
    begin2(new_user)
    items_wait(2)
    new_user = user_total(2, {1: lambda: hop2(0), 2: lambda: hop2(1), 3: lambda: hop2(2)})
    final_user = (usum[...] / (LAYERS + 1)).astype(BF16)
    fu_ref[...] = final_user

    qs[...] = jnp.dot(hot[...], final_user, preferred_element_type=F32).astype(BF16).reshape(2, G // 2, QB, E)
    to_partner = remote(qs.at[other], qp, q_ssem.at[0], q_rsem.at[0], col, partner)
    to_partner.start()
    last2()
    item_parts(2)
    to_partner.wait_recv()
    qt[...] = (qs[c].astype(F32) + qp[...].astype(F32)).astype(BF16)
    for slot, dy, py, px in plane():
        remote(qt.at[py * X + px], qr.at[slot], q_ssem.at[1], q_rsem.at[1], z * Y + py, px * 2 + c).start()
    wait_bytes(qr, q_rsem.at[1])
    total = qt[spot].astype(F32)
    for slot in range(G // 2 - 1):
        total = total + qr[slot].astype(F32)
    qzs[...] = total.astype(BF16)
    for d in (4, 3, 5, 2, 6, 1, 7):
        remote(qzs, qz.at[d - 1], q_ssem.at[2], q_rsem.at[2], zat(d) * Y + y, row).start()
    new_item = item_total(2).astype(BF16)
    final_item = ((isum[...] + new_item.astype(F32)) / (LAYERS + 1)).astype(BF16)
    fi_ref[...] = final_item
    wait_bytes(qz, q_rsem.at[2])
    for d in range(Z - 1):
        total = total + qz[d].astype(F32)
    qall[c, spot] = total.astype(BF16)
    gather_plane(qall, q_ssem.at[3], qg_rsem)
    forward_plane(qall, qg_rsem, q_ssem.at[4], qf_rsem)
    wait_plane(qall, qf_rsem)
    sc_ref[...] = lax.dot_general(qall[...].reshape(NQ, E), final_item, CONTRACT_LANES, preferred_element_type=F32)

    wait_bytes(rs_recv, rs_ssem)
    wait_bytes(cs_recv.at[pl.ds(0, G - 1)], cs_ssem)
    wait_bytes(eu_pan.at[0, pl.ds(0, Z - 1)], eu0_ssem)
    wait_bytes(msend.at[pl.ds(0, Y - 1)], mask_ssem)
    for k in range(LAYERS):
        wait_bytes(ei_pan.at[k, 0, pl.ds(0, G // 2 - 1)], ei_ssem.at[k])
        wait_bytes(ei_pan.at[k, 0], fw_ssem.at[k])
        wait_bytes(pr.at[k], pr_ssem.at[k])
        wait_bytes(ir.at[k], ip_ssem.at[k])
        wait_bytes(up.at[pl.ds(0, 7)], us_ssem.at[k])
        if k:
            wait_bytes(eu_pan.at[k, pl.ds(0, 7)], ag_ssem.at[k])
    to_partner.wait_send()
    wait_bytes(qr, q_ssem.at[1])
    wait_bytes(qz, q_ssem.at[2])
    wait_bytes(qr, q_ssem.at[3])
    wait_bytes(qt, q_ssem.at[4])


def propagate(mask, user, item, queries):
    dma = pltpu.SemaphoreType.DMA
    vmem = pl.BlockSpec(memory_space=pltpu.VMEM)
    L, N = LAYERS, G // 2
    return pl.pallas_call(
        kernel,
        out_shape=(jax.ShapeDtypeStruct((UB, E), BF16), jax.ShapeDtypeStruct((IB, E), BF16),
                   jax.ShapeDtypeStruct((NQ, IB), F32)),
        in_specs=[pl.BlockSpec(memory_space=pl.ANY), vmem, vmem, vmem],
        out_specs=(vmem, vmem, vmem),
        scratch_shapes=[
            pltpu.VMEM((Z, Y * UB, E), jnp.int32),
            pltpu.VMEM((Y, Z, UB, E), BF16),
            pltpu.VMEM((Z, Y - 1, UB, E), BF16),
            pltpu.VMEM((Y, Z, UB, E), BF16),
            pltpu.VMEM((Y, E, Z * UB), BF16),
            pltpu.VMEM((Y, Z, UB), F32),
            pltpu.VMEM((Z * Y - 1, Z, UB), F32),
            pltpu.VMEM((1, E), F32),
            pltpu.VMEM((G, 1, E), F32),
            pltpu.VMEM((Z, UB), F32),
            pltpu.VMEM((Y, 1, E), F32),
            pltpu.VMEM((L, Z, UB, E), BF16),
            pltpu.VMEM((L, 2, N, IB, E), BF16),
            pltpu.VMEM((Z, UB, E), F32),
            pltpu.VMEM((L, 2, 4, UB, E), F32),
            pltpu.VMEM((L, 2, 4, UB, E), F32),
            pltpu.VMEM((L, 2, N, IB, E), F32),
            pltpu.VMEM((L, Y, X, IB, E), F32),
            pltpu.VMEM((L, N, IB, E), F32),
            pltpu.VMEM((L, N - 1, IB, E), F32),
            pltpu.VMEM((NQ, UB), BF16),
            pltpu.VMEM((2, N, QB, E), BF16),
            pltpu.VMEM((N, QB, E), BF16),
            pltpu.VMEM((N, QB, E), BF16),
            pltpu.VMEM((N - 1, QB, E), BF16),
            pltpu.VMEM((Z - 1, QB, E), BF16),
            pltpu.VMEM((QB, E), BF16),
            pltpu.VMEM((2, N, QB, E), BF16),
            pltpu.VMEM((UB, E), F32),
            pltpu.VMEM((IB, E), F32),
            dma((Z,)), dma, dma((Z,)), dma, dma, dma, dma,
            dma, dma, dma((L,)), dma((L, Y)), dma((L,)), dma((L, Y)), dma((L,)), dma((L, 2, 4, 2)),
            dma((L,)), dma((L, Y)), dma((L,)), dma((L,)), dma((L,)), dma((L, 2, 4, 2)),
            dma((5,)), dma((3,)), dma((Y,)), dma((Y,)),
        ],
        compiler_params=pltpu.CompilerParams(collective_id=0, has_side_effects=True, vmem_limit_bytes=60 * 2**20),
    )(mask, user, item, queries.reshape(1, NQ))


def solution(mesh):
    return jax.shard_map(propagate, mesh=mesh,
                         in_specs=(P('row', 'col'), P(('row', 'col'), None), P(('col', 'row'), None), P()),
                         out_specs=(P(('row', 'col'), None), P(('col', 'row'), None), P(None, ('col', 'row'))),
                         check_vma=False)
```

time: 149 us -> 144 us (0.966)
  Pallas kernels: 144 us -> 139 us
    pallas_call x1, Pallas kernels: 144 us -> 139 us  [propagate(): pl.pallas_call(kernel, out_shape=(jax.ShapeDtypeStruct((UB, E), BF16), ja...]
where the time goes in v2:
time: 144 us
  Pallas kernels  139 us (97%)
  local copies, waits for them, and re-layouts  4.67 us (3%)
    pallas_call x1, Pallas kernels, propagate(): pl.pallas_call(kernel, out_shape=(jax.ShapeDtypeStruct((UB, E), BF16), ja...  139 us

profile of v2, /device:TPU:1, one launch (start us, length us, event | category | flops | bytes accessed | tf_op | source)
XLA Modules:
  0.0 144.1 jit_solution(15385519469444466707)
XLA Ops:
  0.6 138.7 %shard_map.67 = (bf16[128,256]{1,0:T(8,128)(2,1)}, bf16[32,256]{1,0:T(8,128)(2,1)}, f32[1024,32]{1,0:T(8,128)}) custom-call(s32[4096,256]{1,0:T(8,128)} %mask_ref.1, bf16[128,256]{1,0:T(8,128)(2,1)} %user_ref.1, bf16[32,256]{1,0:T(8,128)(2,1)} %item_ref.1, s32[1,1024]{1,0:T(1,128)} %bitcast.1), custom_call_target="tpu_custom_call" | custom-call | tf_op jit(solution)/shard_map/pallas_call | solution.py:351
  139.4 1.9 %copy.7 = f32[1024,32]{0,1:T(8,128)} copy(f32[1024,32]{1,0:T(8,128)} %get-tuple-element.5) | data formatting | bytes 262144 | tf_op jit(solution)/shard_map/pallas_call | solution.py:351
  141.3 1.5 %copy.10 = bf16[128,256]{1,0:T(8,128)(2,1)} copy(bf16[128,256]{1,0:T(8,128)(2,1)} %get-tuple-element.9) | data formatting | bytes 131072
  142.7 1.3 copy.11

commit v3 on v2

--- a/solution.py
+++ b/solution.py
@@ -13,7 +13,8 @@
 E = 256
 NQ = 1024
 QB = NQ // G
-H = UB // 2
+NH = 4
+H = UB // NH
 F32, BF16 = jnp.float32, jnp.bfloat16
 MESH = pl.DeviceIdType.MESH
 CONTRACT_ROWS = (((0,), (0,)), ((), ()))
@@ -29,9 +30,9 @@
     pltpu.make_async_copy(ref, ref, sem).wait()
 
 
-def kernel(mask_ref, user_ref, item_ref, query_ref, fu_ref, fi_ref, sc_ref,
+def kernel(mask_ref, user_ref, item_ref, query_ref, fu_ref, fi_ref, qall,
            mask_v, msend, mrecv, adj, adjt, rs_send, rs_recv, cs_send, cs_recv, invu, invi,
-           eu_pan, ei_pan, up, us, ur, ip, pr, iq, ir, hot, qs, qp, qt, qr, qz, qzs, qall, usum, isum,
+           eu_pan, ei_pan, up, us, ur, ip, pr, iq, ir, hot, qs, qp, qt, qr, qz, qzs, usum, isum,
            load_sem, mask_ssem, mask_rsem, rs_ssem, rs_rsem, cs_ssem, cs_rsem,
            eu0_ssem, eu0_rsem, ei_ssem, ei_rsem, fw_ssem, fw_rsem, us_ssem, us_rsem,
            pr_ssem, pr_rsem, ip_ssem, ip_rsem, ag_ssem, ag_rsem, q_ssem, q_rsem, qg_rsem, qf_rsem):
@@ -58,6 +59,8 @@
 
     order = [4, 3, -3, 2, -2, 1, -1, 0]
     piece_of = {d: j for j, d in enumerate(order)}
+    early = (list(range(NH // 2)), list(range(NH // 2, NH)))
+    late = (early[1], early[0])
     right, left = zat(1) * Y + y, zat(-1) * Y + y
 
     loads = []
@@ -158,6 +161,8 @@
                 for cc in range(2):
                     ip[k, cc, s * X + xx] = part[xx, cc]
             remote(ip.at[k, other, pl.ds(s * X, X)], pr.at[k, j], pr_ssem.at[k], pr_rsem.at[k, j], col, partner).start()
+
+    def item_send(k):
         for j, dy in enumerate((2, 1, 3, 0)):
             s = yat(dy)
             wait_bytes(pr.at[k, j], pr_rsem.at[k, j])
@@ -189,48 +194,59 @@
             wait_bytes(pan.at[other, pl.ds(yat(-dy) * X, X)], frsem.at[dy])
 
     def user_total(k, hooks):
-        def send(way, step, h):
+        def emit(way, step, h, first=False):
             rows = pl.ds(h * H, H)
-            remote(us.at[k, way, step, rows], ur.at[k, way, step, rows], us_ssem.at[k], us_rsem.at[k, way, step, h],
-                   right if way == 0 else left, row).start()
-
-        def got(way, step, h):
-            rows = pl.ds(h * H, H)
-            wait_bytes(ur.at[k, way, step, rows], us_rsem.at[k, way, step, h])
-            return ur[k, way, step, h * H:(h + 1) * H]
-
-        def emit(way, step, h, first):
             j = piece_of[4 - step] if way == 0 or step == 0 else piece_of[step - 4]
             value = up[j, h * H:(h + 1) * H]
             if not first:
                 value = value + got(way, step - 1, h)
             us[k, way, step, h * H:(h + 1) * H] = value
-            send(way, step, h)
+            remote(us.at[k, way, step, rows], ur.at[k, way, step, rows], us_ssem.at[k], us_rsem.at[k, way, step, h],
+                   right if way == 0 else left, row).start()
+
+        def got(way, step, h):
+            wait_bytes(ur.at[k, way, step, pl.ds(h * H, H)], us_rsem.at[k, way, step, h])
+            return ur[k, way, step, h * H:(h + 1) * H]
+
+        def hook(*at):
+            if at in hooks:
+                hooks[at]()
 
         user_piece(k, 0)
-        emit(0, 0, 0, True)
-        emit(1, 0, 1, True)
-        user_piece(k, 1)
-        emit(0, 1, 1, True)
-        user_piece(k, 2)
-        emit(1, 1, 0, True)
-        for step in range(1, 4):
-            if step < 3:
-                user_piece(k, 2 * step + 1)
-                user_piece(k, 2 * step + 2)
-            else:
-                user_piece(k, 7)
-            emit(0, step, 0, False)
-            emit(1, step, 1, False)
-            if step < 3:
-                emit(0, step + 1, 1, False)
-                emit(1, step + 1, 0, False)
-            if step in hooks:
-                hooks[step]()
-        halves = []
-        for h in range(2):
-            halves.append(up[7, h * H:(h + 1) * H] + got(0, 3, h) + got(1, 3, h))
-        new_user = jnp.concatenate(halves, axis=0).astype(BF16)
+        for h in range(NH // 2):
+            emit(0, 0, early[0][h], True)
+            emit(1, 0, early[1][h], True)
+        if k == 0:
+            for step in range(1, 4):
+                for way in range(2):
+                    user_piece(k, 2 * step - 1 + way)
+                    for h in early[way] + late[way]:
+                        emit(way, step, h, step == 1 and h in late[way])
+            user_piece(k, 7)
+        else:
+            for way in range(2):
+                user_piece(k, 1 + way)
+                for h in late[way]:
+                    emit(way, 1, h, True)
+            for step in range(1, 4):
+                hook('before', step)
+                if step < 3:
+                    user_piece(k, 2 * step + 1)
+                    user_piece(k, 2 * step + 2)
+                else:
+                    user_piece(k, 7)
+                for h in range(NH // 2):
+                    for way in range(2):
+                        emit(way, step, early[way][h])
+                if step < 3:
+                    for h in range(NH // 2):
+                        for way in range(2):
+                            emit(way, step + 1, late[way][h])
+                hook('after', step)
+        parts = []
+        for h in range(NH):
+            parts.append(up[7, h * H:(h + 1) * H] + got(0, 3, h) + got(1, 3, h))
+        new_user = jnp.concatenate(parts, axis=0).astype(BF16)
         usum[...] += new_user.astype(F32)
         return new_user
 
@@ -245,21 +261,22 @@
 
         def begin(new_user):
             eu_pan[k, z] = new_user
-            for h in range(2):
-                send(0, 0, h)
-                send(1, 0, 1 - h)
+            for h in range(NH):
+                for way in range(2):
+                    send(way, 0, (early[way] + late[way])[h])
 
         def hop(step):
-            for h in range(2):
+            for h in range(NH):
                 for way in range(2):
-                    hh = h if way == 0 else 1 - h
+                    hh = (early[way] + late[way])[h]
                     got(way, step, hh)
-                    if step < 2 or h == 0:
+                    if step < 2 or h < NH // 2:
                         send(way, step + 1, hh)
 
         def last():
-            got(0, 3, 0)
-            got(1, 3, 1)
+            for h in range(NH // 2):
+                for way in range(2):
+                    got(way, 3, early[way][h])
 
         return begin, hop, last
 
@@ -282,30 +299,37 @@
     begin1(new_user)
     wait_bytes(eu_pan.at[0, pl.ds(0, Z - 1)], eu0_rsem)
     item_parts(0)
+    item_send(0)
     for step in range(3):
         hop1(step)
     last1()
     item_parts(1)
     items_next(0)
+    item_send(1)
     items_forward(1)
     items_wait(1)
-    new_user = user_total(1, {2: lambda: items_next(1), 3: lambda: items_forward(2)})
+    new_user = user_total(1, {('after', 1): lambda: items_next(1), ('after', 3): lambda: items_forward(2)})
     begin2, hop2, last2 = gather_user(2)
     begin2(new_user)
     items_wait(2)
-    new_user = user_total(2, {1: lambda: hop2(0), 2: lambda: hop2(1), 3: lambda: hop2(2)})
+
+    def tail2():
+        last2()
+        item_parts(2)
+
+    user_total(2, {('before', 1): lambda: hop2(0), ('before', 2): lambda: hop2(1), ('before', 3): lambda: hop2(2),
+                   ('after', 3): tail2})
     final_user = (usum[...] / (LAYERS + 1)).astype(BF16)
     fu_ref[...] = final_user
 
     qs[...] = jnp.dot(hot[...], final_user, preferred_element_type=F32).astype(BF16).reshape(2, G // 2, QB, E)
     to_partner = remote(qs.at[other], qp, q_ssem.at[0], q_rsem.at[0], col, partner)
     to_partner.start()
-    last2()
-    item_parts(2)
     to_partner.wait_recv()
     qt[...] = (qs[c].astype(F32) + qp[...].astype(F32)).astype(BF16)
     for slot, dy, py, px in plane():
         remote(qt.at[py * X + px], qr.at[slot], q_ssem.at[1], q_rsem.at[1], z * Y + py, px * 2 + c).start()
+    item_send(2)
     wait_bytes(qr, q_rsem.at[1])
     total = qt[spot].astype(F32)
     for slot in range(G // 2 - 1):
@@ -313,17 +337,15 @@
     qzs[...] = total.astype(BF16)
     for d in (4, 3, 5, 2, 6, 1, 7):
         remote(qzs, qz.at[d - 1], q_ssem.at[2], q_rsem.at[2], zat(d) * Y + y, row).start()
-    new_item = item_total(2).astype(BF16)
-    final_item = ((isum[...] + new_item.astype(F32)) / (LAYERS + 1)).astype(BF16)
-    fi_ref[...] = final_item
     wait_bytes(qz, q_rsem.at[2])
     for d in range(Z - 1):
         total = total + qz[d].astype(F32)
     qall[c, spot] = total.astype(BF16)
     gather_plane(qall, q_ssem.at[3], qg_rsem)
+    new_item = item_total(2).astype(BF16)
+    fi_ref[...] = ((isum[...] + new_item.astype(F32)) / (LAYERS + 1)).astype(BF16)
     forward_plane(qall, qg_rsem, q_ssem.at[4], qf_rsem)
     wait_plane(qall, qf_rsem)
-    sc_ref[...] = lax.dot_general(qall[...].reshape(NQ, E), final_item, CONTRACT_LANES, preferred_element_type=F32)
 
     wait_bytes(rs_recv, rs_ssem)
     wait_bytes(cs_recv.at[pl.ds(0, G - 1)], cs_ssem)
@@ -344,14 +366,20 @@
     wait_bytes(qt, q_ssem.at[4])
 
 
+def finish(user_ref, item_ref, picked_ref, fu_ref, fi_ref, sc_ref):
+    fu_ref[...] = user_ref[...]
+    fi_ref[...] = item_ref[...]
+    sc_ref[...] = lax.dot_general(item_ref[...], picked_ref[...], CONTRACT_LANES, preferred_element_type=F32)
+
+
 def propagate(mask, user, item, queries):
     dma = pltpu.SemaphoreType.DMA
     vmem = pl.BlockSpec(memory_space=pltpu.VMEM)
     L, N = LAYERS, G // 2
-    return pl.pallas_call(
+    final_user, final_item, picked = pl.pallas_call(
         kernel,
         out_shape=(jax.ShapeDtypeStruct((UB, E), BF16), jax.ShapeDtypeStruct((IB, E), BF16),
-                   jax.ShapeDtypeStruct((NQ, IB), F32)),
+                   jax.ShapeDtypeStruct((2, N, QB, E), BF16)),
         in_specs=[pl.BlockSpec(memory_space=pl.ANY), vmem, vmem, vmem],
         out_specs=(vmem, vmem, vmem),
         scratch_shapes=[
@@ -382,16 +410,23 @@
             pltpu.VMEM((N - 1, QB, E), BF16),
             pltpu.VMEM((Z - 1, QB, E), BF16),
             pltpu.VMEM((QB, E), BF16),
-            pltpu.VMEM((2, N, QB, E), BF16),
             pltpu.VMEM((UB, E), F32),
             pltpu.VMEM((IB, E), F32),
             dma((Z,)), dma, dma((Z,)), dma, dma, dma, dma,
-            dma, dma, dma((L,)), dma((L, Y)), dma((L,)), dma((L, Y)), dma((L,)), dma((L, 2, 4, 2)),
-            dma((L,)), dma((L, Y)), dma((L,)), dma((L,)), dma((L,)), dma((L, 2, 4, 2)),
+            dma, dma, dma((L,)), dma((L, Y)), dma((L,)), dma((L, Y)), dma((L,)), dma((L, 2, 4, NH)),
+            dma((L,)), dma((L, Y)), dma((L,)), dma((L,)), dma((L,)), dma((L, 2, 4, NH)),
             dma((5,)), dma((3,)), dma((Y,)), dma((Y,)),
         ],
         compiler_params=pltpu.CompilerParams(collective_id=0, has_side_effects=True, vmem_limit_bytes=60 * 2**20),
     )(mask, user, item, queries.reshape(1, NQ))
+    final_user, final_item, scores = pl.pallas_call(
+        finish,
+        out_shape=(jax.ShapeDtypeStruct((UB, E), BF16), jax.ShapeDtypeStruct((IB, E), BF16),
+                   jax.ShapeDtypeStruct((IB, NQ), F32)),
+        in_specs=[vmem, vmem, vmem],
+        out_specs=(vmem, vmem, vmem),
+    )(final_user, final_item, picked.reshape(NQ, E))
+    return final_user, final_item, scores.T
 
 
 def solution(mesh):

time: 144 us -> 125 us (0.87)
  Pallas kernels: 139 us -> 124 us
  local copies, waits for them, and re-layouts: 4.67 us -> 0 us
    pallas_call x1, Pallas kernels: 139 us -> 122 us  [propagate(): pl.pallas_call(kernel, out_shape=(jax.ShapeDtypeStruct((UB, E), BF16), ja...]
    unnamed x2 -> x0, local copies, waits for them, and re-layouts: 2.79 us -> none
    pallas_call x0 -> x1, Pallas kernels: none -> 2.02 us  [propagate(): pl.pallas_call(finish, out_shape=(jax.ShapeDtypeStruct((UB, E), BF16), ja...]
    pallas_call x1 -> x0, local copies, waits for them, and re-layouts: 1.87 us -> none  [propagate(): pl.pallas_call(kernel, out_shape=(jax.ShapeDtypeStruct((UB, E), BF16), ja...]
where the time goes in v3:
time: 125 us
  Pallas kernels  124 us (99%)
    pallas_call x1, Pallas kernels, propagate(): pl.pallas_call(kernel, out_shape=(jax.ShapeDtypeStruct((UB, E), BF16), ja...  122 us

profile of v3, /device:TPU:1, one launch (start us, length us, event | category | flops | bytes accessed | tf_op | source)
XLA Modules:
  0.0 125.0 jit_solution(14397766255644815153)
XLA Ops:
  0.6 122.3 %shard_map.67 = (bf16[128,256]{1,0:T(8,128)(2,1)}, bf16[32,256]{1,0:T(8,128)(2,1)}, bf16[2,16,32,256]{3,2,1,0:T(8,128)(2,1)}) custom-call(s32[4096,256]{1,0:T(8,128)} %mask_ref.1, bf16[128,256]{1,0:T(8,128)(2,1)} %user_ref.1, bf16[32,256]{1,0:T(8,128)(2,1)} %item_ref.1, s32[1,1024]{1,0:T(1,128)} %bitcast.4), custom_call_target="tpu_custom_call" | custom-call | tf_op jit(solution)/shard_map/pallas_call | solution.py:379
  122.9 2.0 %shard_map.68 = (bf16[128,256]{1,0:T(8,128)(2,1)}, bf16[32,256]{1,0:T(8,128)(2,1)}, f32[32,1024]{1,0:T(8,128)}) custom-call(bf16[128,256]{1,0:T(8,128)(2,1)} %get-tuple-element.9.user_ref, bf16[32,256]{1,0:T(8,128)(2,1)} %get-tuple-element.10.item_ref, bf16[1024,256]{1,0:T(8,128)(2,1)} %bitcast.3), custom_call_target="tpu_custom_call" | custom-call | tf_op jit(solution)/shard_map/pallas_call | solution.py:422

commit v4 on v3

--- a/solution.py
+++ b/solution.py
@@ -30,12 +30,12 @@
     pltpu.make_async_copy(ref, ref, sem).wait()
 
 
-def kernel(mask_ref, user_ref, item_ref, query_ref, fu_ref, fi_ref, qall,
+def kernel(mask_ref, user_ref, item_ref, query_ref, fu_hbm, fi_hbm, q_hbm,
            mask_v, msend, mrecv, adj, adjt, rs_send, rs_recv, cs_send, cs_recv, invu, invi,
-           eu_pan, ei_pan, up, us, ur, ip, pr, iq, ir, hot, qs, qp, qt, qr, qz, qzs, usum, isum,
+           eu_pan, ei_pan, up, us, ur, ip, pr, iq, ir, hot, qs, qp, qt, qr, qz, qzs, qall, fu_v, fi_v, usum, isum,
            load_sem, mask_ssem, mask_rsem, rs_ssem, rs_rsem, cs_ssem, cs_rsem,
            eu0_ssem, eu0_rsem, ei_ssem, ei_rsem, fw_ssem, fw_rsem, us_ssem, us_rsem,
-           pr_ssem, pr_rsem, ip_ssem, ip_rsem, ag_ssem, ag_rsem, q_ssem, q_rsem, qg_rsem, qf_rsem):
+           pr_ssem, pr_rsem, ip_ssem, ip_rsem, ag_ssem, ag_rsem, q_ssem, q_rsem, qg_rsem, qf_rsem, out_sem):
     col = lax.axis_index('col')
     row = lax.axis_index('row')
     z, y = lax.div(col, Y), lax.rem(col, Y)
@@ -223,6 +223,7 @@
                     for h in early[way] + late[way]:
                         emit(way, step, h, step == 1 and h in late[way])
             user_piece(k, 7)
+            hook('own')
         else:
             for way in range(2):
                 user_piece(k, 1 + way)
@@ -292,25 +293,29 @@
     def items_wait(k):
         wait_plane(ei_pan.at[k], fw_rsem.at[k])
 
+    def items0():
+        wait_bytes(eu_pan.at[0, pl.ds(0, Z - 1)], eu0_rsem)
+        item_parts(0)
+        item_send(0)
+
     items_forward(0)
     items_wait(0)
-    new_user = user_total(0, {})
+    new_user = user_total(0, {('own',): items0})
     begin1, hop1, last1 = gather_user(1)
     begin1(new_user)
-    wait_bytes(eu_pan.at[0, pl.ds(0, Z - 1)], eu0_rsem)
-    item_parts(0)
-    item_send(0)
-    for step in range(3):
-        hop1(step)
+    hop1(0)
+    hop1(1)
+    items_next(0)
+    hop1(2)
     last1()
     item_parts(1)
-    items_next(0)
+    items_forward(1)
     item_send(1)
-    items_forward(1)
     items_wait(1)
-    new_user = user_total(1, {('after', 1): lambda: items_next(1), ('after', 3): lambda: items_forward(2)})
+    new_user = user_total(1, {('after', 2): lambda: items_next(1)})
     begin2, hop2, last2 = gather_user(2)
     begin2(new_user)
+    items_forward(2)
     items_wait(2)
 
     def tail2():
@@ -320,7 +325,9 @@
     user_total(2, {('before', 1): lambda: hop2(0), ('before', 2): lambda: hop2(1), ('before', 3): lambda: hop2(2),
                    ('after', 3): tail2})
     final_user = (usum[...] / (LAYERS + 1)).astype(BF16)
-    fu_ref[...] = final_user
+    fu_v[...] = final_user
+    outs = [pltpu.make_async_copy(fu_v, fu_hbm, out_sem.at[0])]
+    outs[0].start()
 
     qs[...] = jnp.dot(hot[...], final_user, preferred_element_type=F32).astype(BF16).reshape(2, G // 2, QB, E)
     to_partner = remote(qs.at[other], qp, q_ssem.at[0], q_rsem.at[0], col, partner)
@@ -343,9 +350,15 @@
     qall[c, spot] = total.astype(BF16)
     gather_plane(qall, q_ssem.at[3], qg_rsem)
     new_item = item_total(2).astype(BF16)
-    fi_ref[...] = ((isum[...] + new_item.astype(F32)) / (LAYERS + 1)).astype(BF16)
+    fi_v[...] = ((isum[...] + new_item.astype(F32)) / (LAYERS + 1)).astype(BF16)
+    outs.append(pltpu.make_async_copy(fi_v, fi_hbm, out_sem.at[1]))
+    outs[1].start()
     forward_plane(qall, qg_rsem, q_ssem.at[4], qf_rsem)
+    outs.append(pltpu.make_async_copy(qall.at[c], q_hbm.at[c], out_sem.at[2]))
+    outs[2].start()
     wait_plane(qall, qf_rsem)
+    outs.append(pltpu.make_async_copy(qall.at[other], q_hbm.at[other], out_sem.at[3]))
+    outs[3].start()
 
     wait_bytes(rs_recv, rs_ssem)
     wait_bytes(cs_recv.at[pl.ds(0, G - 1)], cs_ssem)
@@ -364,6 +377,8 @@
     wait_bytes(qz, q_ssem.at[2])
     wait_bytes(qr, q_ssem.at[3])
     wait_bytes(qt, q_ssem.at[4])
+    for out in outs:
+        out.wait()
 
 
 def finish(user_ref, item_ref, picked_ref, fu_ref, fi_ref, sc_ref):
@@ -374,14 +389,14 @@
 
 def propagate(mask, user, item, queries):
     dma = pltpu.SemaphoreType.DMA
-    vmem = pl.BlockSpec(memory_space=pltpu.VMEM)
+    vmem, hbm = pl.BlockSpec(memory_space=pltpu.VMEM), pl.BlockSpec(memory_space=pl.ANY)
     L, N = LAYERS, G // 2
     final_user, final_item, picked = pl.pallas_call(
         kernel,
         out_shape=(jax.ShapeDtypeStruct((UB, E), BF16), jax.ShapeDtypeStruct((IB, E), BF16),
                    jax.ShapeDtypeStruct((2, N, QB, E), BF16)),
-        in_specs=[pl.BlockSpec(memory_space=pl.ANY), vmem, vmem, vmem],
-        out_specs=(vmem, vmem, vmem),
+        in_specs=[hbm, vmem, vmem, vmem],
+        out_specs=(hbm, hbm, hbm),
         scratch_shapes=[
             pltpu.VMEM((Z, Y * UB, E), jnp.int32),
             pltpu.VMEM((Y, Z, UB, E), BF16),
@@ -410,12 +425,15 @@
             pltpu.VMEM((N - 1, QB, E), BF16),
             pltpu.VMEM((Z - 1, QB, E), BF16),
             pltpu.VMEM((QB, E), BF16),
+            pltpu.VMEM((2, N, QB, E), BF16),
+            pltpu.VMEM((UB, E), BF16),
+            pltpu.VMEM((IB, E), BF16),
             pltpu.VMEM((UB, E), F32),
             pltpu.VMEM((IB, E), F32),
             dma((Z,)), dma, dma((Z,)), dma, dma, dma, dma,
             dma, dma, dma((L,)), dma((L, Y)), dma((L,)), dma((L, Y)), dma((L,)), dma((L, 2, 4, NH)),
             dma((L,)), dma((L, Y)), dma((L,)), dma((L,)), dma((L,)), dma((L, 2, 4, NH)),
-            dma((5,)), dma((3,)), dma((Y,)), dma((Y,)),
+            dma((5,)), dma((3,)), dma((Y,)), dma((Y,)), dma((4,)),
         ],
         compiler_params=pltpu.CompilerParams(collective_id=0, has_side_effects=True, vmem_limit_bytes=60 * 2**20),
     )(mask, user, item, queries.reshape(1, NQ))

time: 125 us -> 119 us (0.952)
  Pallas kernels: 124 us -> 118 us
    pallas_call x1, Pallas kernels: 122 us -> 116 us  [propagate(): pl.pallas_call(kernel, out_shape=(jax.ShapeDtypeStruct((UB, E), BF16), ja...]
where the time goes in v4:
time: 119 us
  Pallas kernels  118 us (99%)
    pallas_call x1, Pallas kernels, propagate(): pl.pallas_call(kernel, out_shape=(jax.ShapeDtypeStruct((UB, E), BF16), ja...  116 us

profile of v4, /device:TPU:1, one launch (start us, length us, event | category | flops | bytes accessed | tf_op | source)
XLA Modules:
  0.0 118.8 jit_solution(6415916312939448961)
XLA Ops:
  0.6 116.2 %shard_map.67 = (bf16[128,256]{1,0:T(8,128)(2,1)}, bf16[32,256]{1,0:T(8,128)(2,1)}, bf16[2,16,32,256]{3,2,1,0:T(8,128)(2,1)}) custom-call(s32[4096,256]{1,0:T(8,128)} %mask_ref.1, bf16[128,256]{1,0:T(8,128)(2,1)} %user_ref.1, bf16[32,256]{1,0:T(8,128)(2,1)} %item_ref.1, s32[1,1024]{1,0:T(1,128)} %bitcast.4), custom_call_target="tpu_custom_call" | custom-call | tf_op jit(solution)/shard_map/pallas_call | solution.py:394
  116.8 2.0 %shard_map.68 = (bf16[128,256]{1,0:T(8,128)(2,1)}, bf16[32,256]{1,0:T(8,128)(2,1)}, f32[32,1024]{1,0:T(8,128)}) custom-call(bf16[128,256]{1,0:T(8,128)(2,1)} %get-tuple-element.9.user_ref, bf16[32,256]{1,0:T(8,128)(2,1)} %get-tuple-element.10.item_ref, bf16[1024,256]{1,0:T(8,128)(2,1)} %bitcast.3), custom_call_target="tpu_custom_call" | custom-call | tf_op jit(solution)/shard_map/pallas_call | solution.py:440

commit v5 on v4

--- a/solution.py
+++ b/solution.py
@@ -31,10 +31,9 @@
 
 
 def kernel(mask_ref, user_ref, item_ref, query_ref, fu_hbm, fi_hbm, q_hbm,
-           mask_v, msend, mrecv, adj, adjt, rs_send, rs_recv, cs_send, cs_recv, invu, invi,
+           mask_v, msend, mrecv, adj, adjt, rs_send, rs_y, rs_z, cs_send, cs_row, cs_y, invu, invi,
            eu_pan, ei_pan, up, us, ur, ip, pr, iq, ir, hot, qs, qp, qt, qr, qz, qzs, qall, fu_v, fi_v, usum, isum,
-           load_sem, mask_ssem, mask_rsem, rs_ssem, rs_rsem, cs_ssem, cs_rsem,
-           eu0_ssem, eu0_rsem, ei_ssem, ei_rsem, fw_ssem, fw_rsem, us_ssem, us_rsem,
+           load_sem, mask_ssem, mask_rsem, rs_ssem, rs_rsem, rz_rsem, cs_ssem, cs_rsem, ei_ssem, ei_rsem, fw_ssem, fw_rsem, us_ssem, us_rsem,
            pr_ssem, pr_rsem, ip_ssem, ip_rsem, ag_ssem, ag_rsem, q_ssem, q_rsem, qg_rsem, qf_rsem, out_sem):
     col = lax.axis_index('col')
     row = lax.axis_index('row')
@@ -42,8 +41,7 @@
     x, c = lax.div(row, 2), lax.rem(row, 2)
     other = 1 - c
     partner = x * 2 + other
-    me = y * R + row
-    spot = y * X + x
+    spot = x * Y + y
 
     def zat(d):
         return lax.rem(z + (d % Z), Z)
@@ -51,11 +49,14 @@
     def yat(d):
         return lax.rem(y + (d % Y), Y)
 
+    def xat(d):
+        return lax.rem(x + (d % X), X)
+
     def plane():
-        for dy in (2, 1, 3, 0):
-            for dx in (2, 1, 3, 0):
+        for dx in (2, 1, 3, 0):
+            for dy in (2, 1, 3, 0):
                 if dy or dx:
-                    yield dy * X + dx - 1, dy, yat(dy), lax.rem(x + dx, X)
+                    yield dx * Y + dy - 1, dx, yat(dy), xat(dx)
 
     order = [4, 3, -3, 2, -2, 1, -1, 0]
     piece_of = {d: j for j, d in enumerate(order)}
@@ -71,11 +72,12 @@
         loads.append(load)
 
     barrier = pltpu.get_barrier_semaphore()
-    for d in range(1, Z * Y):
-        pl.semaphore_signal(barrier, inc=1, device_id=(lax.rem(col + d, Z * Y), row), device_id_type=MESH)
-    for dy in range(Y):
-        for dr in range(1, R):
-            pl.semaphore_signal(barrier, inc=1, device_id=(z * Y + yat(dy), lax.rem(row + dr, R)), device_id_type=MESH)
+    for d in range(1, R):
+        pl.semaphore_signal(barrier, inc=1, device_id=(col, lax.rem(row + d, R)), device_id_type=MESH)
+    for d in range(1, Y):
+        pl.semaphore_signal(barrier, inc=1, device_id=(z * Y + yat(d), row), device_id_type=MESH)
+    for peer in (right, left):
+        pl.semaphore_signal(barrier, inc=1, device_id=(peer, row), device_id_type=MESH)
 
     ones_w = jnp.ones((8, E), BF16)
     colsum = jnp.zeros((8, E), F32)
@@ -90,44 +92,111 @@
             rs_send[p, pl.ds(zc, 1), :] = sums[0:1]
             colsum = colsum + jnp.sum(wide.reshape(UB // 8, 8, E), axis=0)
     cs_send[...] = jnp.sum(colsum, axis=0, keepdims=True)
-    cs_recv[me] = cs_send[...]
-    eu_pan[0, z] = user_ref[...]
+    cs_row[row] = cs_send[...]
     ei_pan[0, c, spot] = item_ref[...]
 
-    pl.semaphore_wait(barrier, 31 + 28)
-
-    for dy in range(Y):
-        for dr in range(R):
-            if dy or dr:
-                remote(cs_send, cs_recv.at[me], cs_ssem, cs_rsem, z * Y + yat(dy), lax.rem(row + dr, R)).start()
-    for d in range(1, Z * Y):
-        pc = lax.rem(col + d, Z * Y)
-        remote(rs_send.at[lax.rem(pc, Y)], rs_recv.at[d - 1], rs_ssem, rs_rsem, pc, row).start()
-    for slot, dy, py, px in plane():
-        remote(item_ref, ei_pan.at[0, c, spot], ei_ssem.at[0], ei_rsem.at[0, dy], z * Y + py, px * 2 + c).start()
-    for d in range(1, Z):
-        remote(user_ref, eu_pan.at[0, z], eu0_ssem, eu0_rsem, zat(d) * Y + y, row).start()
-    for j in range(Z):
+    pl.semaphore_wait(barrier, R - 1 + Y - 1 + 2)
+
+    def send_mask(j):
         for d in range(1, Y):
             py = yat(d)
             remote(msend.at[py, j], mrecv.at[j, d - 1], mask_ssem, mask_rsem.at[j], z * Y + py, row).start()
 
+    def gather_user(k):
+        def send(way, step, h):
+            src = eu_pan.at[k, zat(-step if way == 0 else step), pl.ds(h * H, H)]
+            remote(src, src, ag_ssem.at[k], ag_rsem.at[way, step, h], right if way == 0 else left, row).start()
+
+        def got(way, step, h):
+            dst = eu_pan.at[k, zat(-step - 1 if way == 0 else step + 1), pl.ds(h * H, H)]
+            wait_bytes(dst, ag_rsem.at[way, step, h])
+
+        def begin(new_user):
+            eu_pan[k, z] = new_user
+            for h in range(NH):
+                for way in range(2):
+                    send(way, 0, (early[way] + late[way])[h])
+
+        def hop(step):
+            for h in range(NH):
+                for way in range(2):
+                    hh = (early[way] + late[way])[h]
+                    got(way, step, hh)
+                    if step < 2 or h < NH // 2:
+                        send(way, step + 1, hh)
+
+        def last():
+            for h in range(NH // 2):
+                for way in range(2):
+                    got(way, 3, early[way][h])
+
+        return begin, hop, last
+
+    def degree_send(way, step):
+        src = rs_z.at[zat(-step if way == 0 else step)]
+        remote(src, src, rs_ssem.at[1], rz_rsem.at[way, step], right if way == 0 else left, row).start()
+
+    def degree_hop(step):
+        for way in range(2):
+            if step < 3 or way == 0:
+                wait_bytes(rs_z.at[zat(-step - 1 if way == 0 else step + 1)], rz_rsem.at[way, step])
+            if step < 2 or (step < 3 and way == 0):
+                degree_send(way, step + 1)
+
+    for d in range(1, Y):
+        remote(rs_send.at[yat(d)], rs_y.at[d - 1], rs_ssem.at[0], rs_rsem, z * Y + yat(d), row).start()
+    for d in range(1, R):
+        remote(cs_send, cs_row.at[row], cs_ssem.at[0], cs_rsem.at[0], col, lax.rem(row + d, R)).start()
+    for d in range(1, Y):
+        remote(item_ref, ei_pan.at[0, c, spot], ei_ssem.at[0], ei_rsem.at[0, 0], z * Y + yat(d), row).start()
+    send_mask(0)
+    begin0, hop0, last0 = gather_user(0)
+    begin0(user_ref[...])
+    send_mask(1)
+
     usum[...] = user_ref[...].astype(F32)
     isum[...] = item_ref[...].astype(F32)
+    wait_bytes(rs_y, rs_rsem)
+    rs_z[z] = rs_send[y] + rs_y[0] + rs_y[1] + rs_y[2]
+    for way in range(2):
+        degree_send(way, 0)
+
+    wait_bytes(ei_pan.at[0, c, pl.ds(0, Y - 1)], ei_rsem.at[0, 0])
+    own = ei_pan.at[0, c, pl.ds(x * Y, Y)]
+    for d in range(1, X):
+        remote(own, own, ei_ssem.at[0], ei_rsem.at[0, d], col, xat(d) * 2 + c).start()
+    remote(own, own, fw_ssem.at[0], fw_rsem.at[0, 0], col, partner).start()
+
+    wait_bytes(cs_row.at[pl.ds(0, R - 1)], cs_rsem.at[0])
+    deg = cs_row[0]
+    for r in range(1, R):
+        deg = deg + cs_row[r]
+    cs_y[y] = deg
+    for d in range(1, Y):
+        remote(cs_y.at[y], cs_y.at[y], cs_ssem.at[1], cs_rsem.at[1], z * Y + yat(d), row).start()
+    for j in range(2, Z):
+        send_mask(j)
+
     base = (row * (Z * Y) + col) * UB
     ids = lax.broadcasted_iota(jnp.int32, (UB, NQ), 0) + base
     hot[...] = jnp.where(ids == query_ref[...], 1.0, 0.0).T.astype(BF16)
 
-    wait_bytes(cs_recv.at[pl.ds(0, G - 1)], cs_rsem)
+    degree_hop(0)
+    degree_hop(1)
+    hop0(0)
+    degree_hop(2)
+    hop0(1)
+    for d in (1, 3, 2):
+        rows = pl.ds(xat(-d) * Y, Y)
+        wait_bytes(ei_pan.at[0, c, rows], ei_rsem.at[0, d])
+        remote(ei_pan.at[0, c, rows], ei_pan.at[0, c, rows], fw_ssem.at[0], fw_rsem.at[0, d], col, partner).start()
+    wait_bytes(cs_y.at[pl.ds(0, Y - 1)], cs_rsem.at[1])
     for s in range(Y):
-        deg = cs_recv[s * R]
-        for r in range(1, R):
-            deg = deg + cs_recv[s * R + r]
-        invi[s] = lax.rsqrt(jnp.maximum(deg, 1.0))
-    wait_bytes(rs_recv, rs_rsem)
-    deg = rs_send[y]
-    for d in range(Z * Y - 1):
-        deg = deg + rs_recv[d]
+        invi[s] = lax.rsqrt(jnp.maximum(cs_y[s], 1.0))
+    degree_hop(3)
+    deg = rs_z[0]
+    for d in range(1, Z):
+        deg = deg + rs_z[d]
     invu[...] = lax.rsqrt(jnp.maximum(deg, 1.0))
 
     def make_adj(j, zc):
@@ -147,7 +216,7 @@
             make_adj(j, zc)
         acc = None
         for s in range(Y):
-            panel = jnp.concatenate([ei_pan[k, cc, s * X + xx] for xx in range(X) for cc in range(2)], axis=0)
+            panel = jnp.concatenate([ei_pan[k, cc, xx * Y + s] for xx in range(X) for cc in range(2)], axis=0)
             t = jnp.dot(adj[s, zc], panel, preferred_element_type=F32)
             acc = t if acc is None else acc + t
         up[j] = acc
@@ -167,31 +236,32 @@
             s = yat(dy)
             wait_bytes(pr.at[k, j], pr_rsem.at[k, j])
             iq[k, pl.ds(s * X, X)] = ip[k, c, pl.ds(s * X, X)] + pr[k, j]
-            for slot, dy2, py, px in plane():
-                if dy2 == dy:
-                    remote(iq.at[k, s * X + px], ir.at[k, slot], ip_ssem.at[k], ip_rsem.at[k], z * Y + py, px * 2 + c).start()
+            for dx in (2, 1, 3, 0):
+                if dy or dx:
+                    px = xat(dx)
+                    remote(iq.at[k, s * X + px], ir.at[k, dy * X + dx - 1], ip_ssem.at[k], ip_rsem.at[k],
+                           z * Y + s, px * 2 + c).start()
 
     def item_total(k):
         wait_bytes(ir.at[k], ip_rsem.at[k])
-        total = iq[k, spot]
+        total = iq[k, y * X + x]
         for slot in range(G // 2 - 1):
             total = total + ir[k, slot]
         return total
 
     def gather_plane(pan, ssem, rsem):
-        for slot, dy, py, px in plane():
-            remote(pan.at[c, spot], pan.at[c, spot], ssem, rsem.at[dy], z * Y + py, px * 2 + c).start()
+        for slot, dx, py, px in plane():
+            remote(pan.at[c, spot], pan.at[c, spot], ssem, rsem.at[dx], z * Y + py, px * 2 + c).start()
 
     def forward_plane(pan, rsem, fssem, frsem):
-        for dy in (0, 1, 3, 2):
-            n = X - 1 if dy == 0 else X
-            rows = pl.ds(yat(-dy) * X, X)
-            wait_bytes(pan.at[c, pl.ds(0, n)], rsem.at[dy])
-            remote(pan.at[c, rows], pan.at[c, rows], fssem, frsem.at[dy], col, partner).start()
+        for dx in (0, 1, 3, 2):
+            rows = pl.ds(xat(-dx) * Y, Y)
+            wait_bytes(pan.at[c, pl.ds(0, Y if dx else Y - 1)], rsem.at[dx])
+            remote(pan.at[c, rows], pan.at[c, rows], fssem, frsem.at[dx], col, partner).start()
 
     def wait_plane(pan, frsem):
-        for dy in (0, 1, 3, 2):
-            wait_bytes(pan.at[other, pl.ds(yat(-dy) * X, X)], frsem.at[dy])
+        for dx in (0, 1, 3, 2):
+            wait_bytes(pan.at[other, pl.ds(xat(-dx) * Y, Y)], frsem.at[dx])
 
     def user_total(k, hooks):
         def emit(way, step, h, first=False):
@@ -201,11 +271,11 @@
             if not first:
                 value = value + got(way, step - 1, h)
             us[k, way, step, h * H:(h + 1) * H] = value
-            remote(us.at[k, way, step, rows], ur.at[k, way, step, rows], us_ssem.at[k], us_rsem.at[k, way, step, h],
+            remote(us.at[k, way, step, rows], ur.at[k, way, step, rows], us_ssem.at[k], us_rsem.at[way, step, h],
                    right if way == 0 else left, row).start()
 
         def got(way, step, h):
-            wait_bytes(ur.at[k, way, step, pl.ds(h * H, H)], us_rsem.at[k, way, step, h])
+            wait_bytes(ur.at[k, way, step, pl.ds(h * H, H)], us_rsem.at[way, step, h])
             return ur[k, way, step, h * H:(h + 1) * H]
 
         def hook(*at):
@@ -217,11 +287,13 @@
             emit(0, 0, early[0][h], True)
             emit(1, 0, early[1][h], True)
         if k == 0:
+            hook('piece', 0)
             for step in range(1, 4):
                 for way in range(2):
                     user_piece(k, 2 * step - 1 + way)
                     for h in early[way] + late[way]:
                         emit(way, step, h, step == 1 and h in late[way])
+                hook('piece', step)
             user_piece(k, 7)
             hook('own')
         else:
@@ -251,36 +323,6 @@
         usum[...] += new_user.astype(F32)
         return new_user
 
-    def gather_user(k):
-        def send(way, step, h):
-            src = eu_pan.at[k, zat(-step if way == 0 else step), pl.ds(h * H, H)]
-            remote(src, src, ag_ssem.at[k], ag_rsem.at[k, way, step, h], right if way == 0 else left, row).start()
-
-        def got(way, step, h):
-            dst = eu_pan.at[k, zat(-step - 1 if way == 0 else step + 1), pl.ds(h * H, H)]
-            wait_bytes(dst, ag_rsem.at[k, way, step, h])
-
-        def begin(new_user):
-            eu_pan[k, z] = new_user
-            for h in range(NH):
-                for way in range(2):
-                    send(way, 0, (early[way] + late[way])[h])
-
-        def hop(step):
-            for h in range(NH):
-                for way in range(2):
-                    hh = (early[way] + late[way])[h]
-                    got(way, step, hh)
-                    if step < 2 or h < NH // 2:
-                        send(way, step + 1, hh)
-
-        def last():
-            for h in range(NH // 2):
-                for way in range(2):
-                    got(way, 3, early[way][h])
-
-        return begin, hop, last
-
     def items_next(k):
         new_item = item_total(k).astype(BF16)
         isum[...] += new_item.astype(F32)
@@ -294,13 +336,11 @@
         wait_plane(ei_pan.at[k], fw_rsem.at[k])
 
     def items0():
-        wait_bytes(eu_pan.at[0, pl.ds(0, Z - 1)], eu0_rsem)
         item_parts(0)
         item_send(0)
 
-    items_forward(0)
     items_wait(0)
-    new_user = user_total(0, {('own',): items0})
+    new_user = user_total(0, {('piece', 0): lambda: hop0(2), ('piece', 1): last0, ('own',): items0})
     begin1, hop1, last1 = gather_user(1)
     begin1(new_user)
     hop1(0)
@@ -334,8 +374,8 @@
     to_partner.start()
     to_partner.wait_recv()
     qt[...] = (qs[c].astype(F32) + qp[...].astype(F32)).astype(BF16)
-    for slot, dy, py, px in plane():
-        remote(qt.at[py * X + px], qr.at[slot], q_ssem.at[1], q_rsem.at[1], z * Y + py, px * 2 + c).start()
+    for slot, dx, py, px in plane():
+        remote(qt.at[px * Y + py], qr.at[slot], q_ssem.at[1], q_rsem.at[1], z * Y + py, px * 2 + c).start()
     item_send(2)
     wait_bytes(qr, q_rsem.at[1])
     total = qt[spot].astype(F32)
@@ -360,9 +400,10 @@
     outs.append(pltpu.make_async_copy(qall.at[other], q_hbm.at[other], out_sem.at[3]))
     outs[3].start()
 
-    wait_bytes(rs_recv, rs_ssem)
-    wait_bytes(cs_recv.at[pl.ds(0, G - 1)], cs_ssem)
-    wait_bytes(eu_pan.at[0, pl.ds(0, Z - 1)], eu0_ssem)
+    wait_bytes(rs_y, rs_ssem.at[0])
+    wait_bytes(rs_z.at[pl.ds(0, Z - 1)], rs_ssem.at[1])
+    wait_bytes(cs_row.at[pl.ds(0, R - 1)], cs_ssem.at[0])
+    wait_bytes(cs_y.at[pl.ds(0, Y - 1)], cs_ssem.at[1])
     wait_bytes(msend.at[pl.ds(0, Y - 1)], mask_ssem)
     for k in range(LAYERS):
         wait_bytes(ei_pan.at[k, 0, pl.ds(0, G // 2 - 1)], ei_ssem.at[k])
@@ -370,8 +411,7 @@
         wait_bytes(pr.at[k], pr_ssem.at[k])
         wait_bytes(ir.at[k], ip_ssem.at[k])
         wait_bytes(up.at[pl.ds(0, 7)], us_ssem.at[k])
-        if k:
-            wait_bytes(eu_pan.at[k, pl.ds(0, 7)], ag_ssem.at[k])
+        wait_bytes(eu_pan.at[k, pl.ds(0, 7)], ag_ssem.at[k])
     to_partner.wait_send()
     wait_bytes(qr, q_ssem.at[1])
     wait_bytes(qz, q_ssem.at[2])
@@ -404,9 +444,11 @@
             pltpu.VMEM((Y, Z, UB, E), BF16),
             pltpu.VMEM((Y, E, Z * UB), BF16),
             pltpu.VMEM((Y, Z, UB), F32),
-            pltpu.VMEM((Z * Y - 1, Z, UB), F32),
+            pltpu.VMEM((Y - 1, Z, UB), F32),
+            pltpu.VMEM((Z, Z, UB), F32),
             pltpu.VMEM((1, E), F32),
-            pltpu.VMEM((G, 1, E), F32),
+            pltpu.VMEM((R, 1, E), F32),
+            pltpu.VMEM((Y, 1, E), F32),
             pltpu.VMEM((Z, UB), F32),
             pltpu.VMEM((Y, 1, E), F32),
             pltpu.VMEM((L, Z, UB, E), BF16),
@@ -430,10 +472,15 @@
             pltpu.VMEM((IB, E), BF16),
             pltpu.VMEM((UB, E), F32),
             pltpu.VMEM((IB, E), F32),
-            dma((Z,)), dma, dma((Z,)), dma, dma, dma, dma,
-            dma, dma, dma((L,)), dma((L, Y)), dma((L,)), dma((L, Y)), dma((L,)), dma((L, 2, 4, NH)),
-            dma((L,)), dma((L, Y)), dma((L,)), dma((L,)), dma((L,)), dma((L, 2, 4, NH)),
-            dma((5,)), dma((3,)), dma((Y,)), dma((Y,)), dma((4,)),
+            dma((Z,)), dma, dma((Z,)),
+            dma((2,)), dma, dma((2, 4)),
+            dma((2,)), dma((2,)),
+            dma((L,)), dma((L, X)), dma((L,)), dma((L, X)),
+            dma((L,)), dma((2, 4, NH)),
+            dma((L,)), dma((L, Y)), dma((L,)), dma((L,)),
+            dma((L,)), dma((2, 4, NH)),
+            dma((5,)), dma((3,)), dma((X,)), dma((X,)),
+            dma((4,)),
         ],
         compiler_params=pltpu.CompilerParams(collective_id=0, has_side_effects=True, vmem_limit_bytes=60 * 2**20),
     )(mask, user, item, queries.reshape(1, NQ))

time: 119 us -> 118 us (level)
  no operation moved by 1% of the time
where the time goes in v5:
time: 118 us
  Pallas kernels  118 us (100%)
    pallas_call x1, Pallas kernels, propagate(): pl.pallas_call(kernel, out_shape=(jax.ShapeDtypeStruct((UB, E), BF16), ja...  116 us

profile of v5, /device:TPU:1, one launch (start us, length us, event | category | flops | bytes accessed | tf_op | source)
XLA Modules:
  0.0 118.3 jit_solution(2001391893406049732)
XLA Ops:
  0.6 115.6 %shard_map.67 = (bf16[128,256]{1,0:T(8,128)(2,1)}, bf16[32,256]{1,0:T(8,128)(2,1)}, bf16[2,16,32,256]{3,2,1,0:T(8,128)(2,1)}) custom-call(s32[4096,256]{1,0:T(8,128)} %mask_ref.1, bf16[128,256]{1,0:T(8,128)(2,1)} %user_ref.1, bf16[32,256]{1,0:T(8,128)(2,1)} %item_ref.1, s32[1,1024]{1,0:T(1,128)} %bitcast.4), custom_call_target="tpu_custom_call" | custom-call | tf_op jit(solution)/shard_map/pallas_call | solution.py:434
  116.2 2.0 %shard_map.68 = (bf16[128,256]{1,0:T(8,128)(2,1)}, bf16[32,256]{1,0:T(8,128)(2,1)}, f32[32,1024]{1,0:T(8,128)}) custom-call(bf16[128,256]{1,0:T(8,128)(2,1)} %get-tuple-element.9.user_ref, bf16[32,256]{1,0:T(8,128)(2,1)} %get-tuple-element.10.item_ref, bf16[1024,256]{1,0:T(8,128)(2,1)} %bitcast.3), custom_call_target="tpu_custom_call" | custom-call | tf_op jit(solution)/shard_map/pallas_call | solution.py:487

commit v6 on v5

--- a/solution.py
+++ b/solution.py
@@ -32,7 +32,7 @@
 
 def kernel(mask_ref, user_ref, item_ref, query_ref, fu_hbm, fi_hbm, q_hbm,
            mask_v, msend, mrecv, adj, adjt, rs_send, rs_y, rs_z, cs_send, cs_row, cs_y, invu, invi,
-           eu_pan, ei_pan, up, us, ur, ip, pr, iq, ir, hot, qs, qp, qt, qr, qz, qzs, qall, fu_v, fi_v, usum, isum,
+           eu_pan, ei_pan, up, macc, us, ur, ip, pr, iq, ir, hot, qs, qp, qt, qr, qz, qzs, qall, fu_v, fi_v, usum, isum,
            load_sem, mask_ssem, mask_rsem, rs_ssem, rs_rsem, rz_rsem, cs_ssem, cs_rsem, ei_ssem, ei_rsem, fw_ssem, fw_rsem, us_ssem, us_rsem,
            pr_ssem, pr_rsem, ip_ssem, ip_rsem, ag_ssem, ag_rsem, q_ssem, q_rsem, qg_rsem, qf_rsem, out_sem):
     col = lax.axis_index('col')
@@ -76,8 +76,8 @@
         pl.semaphore_signal(barrier, inc=1, device_id=(col, lax.rem(row + d, R)), device_id_type=MESH)
     for d in range(1, Y):
         pl.semaphore_signal(barrier, inc=1, device_id=(z * Y + yat(d), row), device_id_type=MESH)
-    for peer in (right, left):
-        pl.semaphore_signal(barrier, inc=1, device_id=(peer, row), device_id_type=MESH)
+    for d in range(1, Z):
+        pl.semaphore_signal(barrier, inc=1, device_id=(zat(d) * Y + y, row), device_id_type=MESH)
 
     ones_w = jnp.ones((8, E), BF16)
     colsum = jnp.zeros((8, E), F32)
@@ -95,7 +95,7 @@
     cs_row[row] = cs_send[...]
     ei_pan[0, c, spot] = item_ref[...]
 
-    pl.semaphore_wait(barrier, R - 1 + Y - 1 + 2)
+    pl.semaphore_wait(barrier, R - 1 + Y - 1 + Z - 1)
 
     def send_mask(j):
         for d in range(1, Y):
@@ -131,17 +131,6 @@
                     got(way, 3, early[way][h])
 
         return begin, hop, last
-
-    def degree_send(way, step):
-        src = rs_z.at[zat(-step if way == 0 else step)]
-        remote(src, src, rs_ssem.at[1], rz_rsem.at[way, step], right if way == 0 else left, row).start()
-
-    def degree_hop(step):
-        for way in range(2):
-            if step < 3 or way == 0:
-                wait_bytes(rs_z.at[zat(-step - 1 if way == 0 else step + 1)], rz_rsem.at[way, step])
-            if step < 2 or (step < 3 and way == 0):
-                degree_send(way, step + 1)
 
     for d in range(1, Y):
         remote(rs_send.at[yat(d)], rs_y.at[d - 1], rs_ssem.at[0], rs_rsem, z * Y + yat(d), row).start()
@@ -158,8 +147,8 @@
     isum[...] = item_ref[...].astype(F32)
     wait_bytes(rs_y, rs_rsem)
     rs_z[z] = rs_send[y] + rs_y[0] + rs_y[1] + rs_y[2]
-    for way in range(2):
-        degree_send(way, 0)
+    for d in (4, 3, 5, 2, 6, 1, 7):
+        remote(rs_z.at[z], rs_z.at[z], rs_ssem.at[1], rz_rsem, zat(d) * Y + y, row).start()
 
     wait_bytes(ei_pan.at[0, c, pl.ds(0, Y - 1)], ei_rsem.at[0, 0])
     own = ei_pan.at[0, c, pl.ds(x * Y, Y)]
@@ -181,11 +170,7 @@
     ids = lax.broadcasted_iota(jnp.int32, (UB, NQ), 0) + base
     hot[...] = jnp.where(ids == query_ref[...], 1.0, 0.0).T.astype(BF16)
 
-    degree_hop(0)
-    degree_hop(1)
     hop0(0)
-    degree_hop(2)
-    hop0(1)
     for d in (1, 3, 2):
         rows = pl.ds(xat(-d) * Y, Y)
         wait_bytes(ei_pan.at[0, c, rows], ei_rsem.at[0, d])
@@ -193,7 +178,7 @@
     wait_bytes(cs_y.at[pl.ds(0, Y - 1)], cs_rsem.at[1])
     for s in range(Y):
         invi[s] = lax.rsqrt(jnp.maximum(cs_y[s], 1.0))
-    degree_hop(3)
+    wait_bytes(rs_z.at[pl.ds(0, Z - 1)], rz_rsem)
     deg = rs_z[0]
     for d in range(1, Z):
         deg = deg + rs_z[d]
@@ -221,15 +206,33 @@
             acc = t if acc is None else acc + t
         up[j] = acc
 
-    def item_parts(k):
-        eu = eu_pan[k].reshape(Z * UB, E)
+    def item_share(k, product):
         for j, dy in enumerate((2, 1, 3, 0)):
             s = yat(dy)
-            part = jnp.dot(adjt[s], eu, preferred_element_type=F32).reshape(X, 2, IB, E)
+            part = product(s).reshape(X, 2, IB, E)
             for xx in range(X):
                 for cc in range(2):
                     ip[k, cc, s * X + xx] = part[xx, cc]
             remote(ip.at[k, other, pl.ds(s * X, X)], pr.at[k, j], pr_ssem.at[k], pr_rsem.at[k, j], col, partner).start()
+
+    def item_parts(k):
+        eu = eu_pan[k].reshape(Z * UB, E)
+        item_share(k, lambda s: jnp.dot(adjt[s], eu, preferred_element_type=F32))
+
+    def item_pair(n):
+        near = [zat(d) for d in ((0, 1), (-1, 2), (-2, 3), (-3, 4))[n]]
+        eu = jnp.concatenate([eu_pan[1, zc] for zc in near], axis=0)
+
+        def add(s):
+            lhs = jnp.concatenate([adjt[s, :, pl.ds(pl.multiple_of(zc * UB, UB), UB)] for zc in near], axis=1)
+            part = jnp.dot(lhs, eu, preferred_element_type=F32)
+            return part + macc[s] if n else part
+
+        if n < 3:
+            for s in range(Y):
+                macc[s] = add(s)
+        else:
+            item_share(1, add)
 
     def item_send(k):
         for j, dy in enumerate((2, 1, 3, 0)):
@@ -339,16 +342,20 @@
         item_parts(0)
         item_send(0)
 
+    hop0(1)
     items_wait(0)
     new_user = user_total(0, {('piece', 0): lambda: hop0(2), ('piece', 1): last0, ('own',): items0})
     begin1, hop1, last1 = gather_user(1)
     begin1(new_user)
     hop1(0)
+    item_pair(0)
     hop1(1)
+    item_pair(1)
     items_next(0)
     hop1(2)
+    item_pair(2)
     last1()
-    item_parts(1)
+    item_pair(3)
     items_forward(1)
     item_send(1)
     items_wait(1)
@@ -358,12 +365,7 @@
     items_forward(2)
     items_wait(2)
 
-    def tail2():
-        last2()
-        item_parts(2)
-
-    user_total(2, {('before', 1): lambda: hop2(0), ('before', 2): lambda: hop2(1), ('before', 3): lambda: hop2(2),
-                   ('after', 3): tail2})
+    user_total(2, {('after', 1): lambda: hop2(0), ('after', 2): lambda: hop2(1), ('after', 3): lambda: hop2(2)})
     final_user = (usum[...] / (LAYERS + 1)).astype(BF16)
     fu_v[...] = final_user
     outs = [pltpu.make_async_copy(fu_v, fu_hbm, out_sem.at[0])]
@@ -376,6 +378,8 @@
     qt[...] = (qs[c].astype(F32) + qp[...].astype(F32)).astype(BF16)
     for slot, dx, py, px in plane():
         remote(qt.at[px * Y + py], qr.at[slot], q_ssem.at[1], q_rsem.at[1], z * Y + py, px * 2 + c).start()
+    last2()
+    item_parts(2)
     item_send(2)
     wait_bytes(qr, q_rsem.at[1])
     total = qt[spot].astype(F32)
@@ -454,6 +458,7 @@
             pltpu.VMEM((L, Z, UB, E), BF16),
             pltpu.VMEM((L, 2, N, IB, E), BF16),
             pltpu.VMEM((Z, UB, E), F32),
+            pltpu.VMEM((Y, E, E), F32),
             pltpu.VMEM((L, 2, 4, UB, E), F32),
             pltpu.VMEM((L, 2, 4, UB, E), F32),
             pltpu.VMEM((L, 2, N, IB, E), F32),
@@ -473,7 +478,7 @@
             pltpu.VMEM((UB, E), F32),
             pltpu.VMEM((IB, E), F32),
             dma((Z,)), dma, dma((Z,)),
-            dma((2,)), dma, dma((2, 4)),
+            dma((2,)), dma, dma,
             dma((2,)), dma((2,)),
             dma((L,)), dma((L, X)), dma((L,)), dma((L, X)),
             dma((L,)), dma((2, 4, NH)),

time: 118 us -> 114 us (0.966)
  Pallas kernels: 118 us -> 114 us
    pallas_call x1, Pallas kernels: 116 us -> 112 us  [propagate(): pl.pallas_call(kernel, out_shape=(jax.ShapeDtypeStruct((UB, E), BF16), ja...]
where the time goes in v6:
time: 114 us
  Pallas kernels  114 us (100%)
    pallas_call x1, Pallas kernels, propagate(): pl.pallas_call(kernel, out_shape=(jax.ShapeDtypeStruct((UB, E), BF16), ja...  112 us

profile of v6, /device:TPU:1, one launch (start us, length us, event | category | flops | bytes accessed | tf_op | source)
XLA Modules:
  0.0 114.3 jit_solution(17536854764234152329)
XLA Ops:
  0.6 111.7 %shard_map.67 = (bf16[128,256]{1,0:T(8,128)(2,1)}, bf16[32,256]{1,0:T(8,128)(2,1)}, bf16[2,16,32,256]{3,2,1,0:T(8,128)(2,1)}) custom-call(s32[4096,256]{1,0:T(8,128)} %mask_ref.1, bf16[128,256]{1,0:T(8,128)(2,1)} %user_ref.1, bf16[32,256]{1,0:T(8,128)(2,1)} %item_ref.1, s32[1,1024]{1,0:T(1,128)} %bitcast.4), custom_call_target="tpu_custom_call" | custom-call | tf_op jit(solution)/shard_map/pallas_call | solution.py:438
  112.3 2.0 %shard_map.68 = (bf16[128,256]{1,0:T(8,128)(2,1)}, bf16[32,256]{1,0:T(8,128)(2,1)}, f32[32,1024]{1,0:T(8,128)}) custom-call(bf16[128,256]{1,0:T(8,128)(2,1)} %get-tuple-element.9.user_ref, bf16[32,256]{1,0:T(8,128)(2,1)} %get-tuple-element.10.item_ref, bf16[1024,256]{1,0:T(8,128)(2,1)} %bitcast.3), custom_call_target="tpu_custom_call" | custom-call | tf_op jit(solution)/shard_map/pallas_call | solution.py:492

commit v7 on v6

--- a/solution.py
+++ b/solution.py
@@ -30,8 +30,8 @@
     pltpu.make_async_copy(ref, ref, sem).wait()
 
 
-def kernel(mask_ref, user_ref, item_ref, query_ref, fu_hbm, fi_hbm, q_hbm,
-           mask_v, msend, mrecv, adj, adjt, rs_send, rs_y, rs_z, cs_send, cs_row, cs_y, invu, invi,
+def kernel(mask_ref, user_hbm, item_hbm, query_hbm, fu_out, fi_out, q_out,
+           mask_v, user_ref, item_ref, query_ref, msend, mrecv, adj, adjt, rs_send, rs_y, rs_z, cs_send, cs_row, cs_y, invu, invi,
            eu_pan, ei_pan, up, macc, us, ur, ip, pr, iq, ir, hot, qs, qp, qt, qr, qz, qzs, qall, fu_v, fi_v, usum, isum,
            load_sem, mask_ssem, mask_rsem, rs_ssem, rs_rsem, rz_rsem, cs_ssem, cs_rsem, ei_ssem, ei_rsem, fw_ssem, fw_rsem, us_ssem, us_rsem,
            pr_ssem, pr_rsem, ip_ssem, ip_rsem, ag_ssem, ag_rsem, q_ssem, q_rsem, qg_rsem, qf_rsem, out_sem):
@@ -60,6 +60,17 @@
 
     order = [4, 3, -3, 2, -2, 1, -1, 0]
     piece_of = {d: j for j, d in enumerate(order)}
+    place = lax.rem(z, Z // 2)
+
+    def ring_order(step, run):
+        if step == 0:
+            pl.when(place == 0)(lambda: run(((1,), (0,))))
+            pl.when(place == Z // 2 - 1)(lambda: run(((0,), (1,))))
+            pl.when((place > 0) & (place < Z // 2 - 1))(lambda: run(((0, 1),)))
+        else:
+            pl.when(place < Z // 4)(lambda: run(((1,), (0,))))
+            pl.when(place >= Z // 4)(lambda: run(((0,), (1,))))
+
     early = (list(range(NH // 2)), list(range(NH // 2, NH)))
     late = (early[1], early[0])
     right, left = zat(1) * Y + y, zat(-1) * Y + y
@@ -70,6 +81,11 @@
         load = pltpu.make_async_copy(mask_ref.at[pl.ds(zc * (Y * UB), Y * UB)], mask_v.at[j], load_sem.at[j])
         load.start()
         loads.append(load)
+
+    small = []
+    for i, (src, dst) in enumerate(((user_hbm, user_ref), (item_hbm, item_ref), (query_hbm, query_ref))):
+        small.append(pltpu.make_async_copy(src, dst, load_sem.at[Z + i]))
+        small[i].start()
 
     barrier = pltpu.get_barrier_semaphore()
     for d in range(1, R):
@@ -81,9 +97,18 @@
 
     ones_w = jnp.ones((8, E), BF16)
     colsum = jnp.zeros((8, E), F32)
+
+    def send_mask(j):
+        for d in range(1, Y):
+            py = yat(d)
+            remote(msend.at[py, j], mrecv.at[j, d - 1], mask_ssem, mask_rsem.at[j], z * Y + py, row).start()
+
     for j, d in enumerate(order):
         zc = zat(d)
         loads[j].wait()
+        if j == 1:
+            pl.semaphore_wait(barrier, R - 1 + Y - 1 + Z - 1)
+            send_mask(0)
         for p in range(Y):
             wide = mask_v[j, p * UB:(p + 1) * UB, :].astype(F32)
             block = wide.astype(BF16)
@@ -93,14 +118,9 @@
             colsum = colsum + jnp.sum(wide.reshape(UB // 8, 8, E), axis=0)
     cs_send[...] = jnp.sum(colsum, axis=0, keepdims=True)
     cs_row[row] = cs_send[...]
+    for load in small:
+        load.wait()
     ei_pan[0, c, spot] = item_ref[...]
-
-    pl.semaphore_wait(barrier, R - 1 + Y - 1 + Z - 1)
-
-    def send_mask(j):
-        for d in range(1, Y):
-            py = yat(d)
-            remote(msend.at[py, j], mrecv.at[j, d - 1], mask_ssem, mask_rsem.at[j], z * Y + py, row).start()
 
     def gather_user(k):
         def send(way, step, h):
@@ -118,12 +138,16 @@
                     send(way, 0, (early[way] + late[way])[h])
 
         def hop(step):
-            for h in range(NH):
-                for way in range(2):
-                    hh = (early[way] + late[way])[h]
-                    got(way, step, hh)
-                    if step < 2 or h < NH // 2:
-                        send(way, step + 1, hh)
+            def run(groups):
+                for ways in groups:
+                    for h in range(NH):
+                        for way in ways:
+                            hh = (early[way] + late[way])[h]
+                            got(way, step, hh)
+                            if step < 2 or h < NH // 2:
+                                send(way, step + 1, hh)
+
+            ring_order(step, run)
 
         def last():
             for h in range(NH // 2):
@@ -138,7 +162,6 @@
         remote(cs_send, cs_row.at[row], cs_ssem.at[0], cs_rsem.at[0], col, lax.rem(row + d, R)).start()
     for d in range(1, Y):
         remote(item_ref, ei_pan.at[0, c, spot], ei_ssem.at[0], ei_rsem.at[0, 0], z * Y + yat(d), row).start()
-    send_mask(0)
     begin0, hop0, last0 = gather_user(0)
     begin0(user_ref[...])
     send_mask(1)
@@ -206,7 +229,7 @@
             acc = t if acc is None else acc + t
         up[j] = acc
 
-    def item_share(k, product):
+    def item_share(k, product, lag=Y):
         for j, dy in enumerate((2, 1, 3, 0)):
             s = yat(dy)
             part = product(s).reshape(X, 2, IB, E)
@@ -214,10 +237,12 @@
                 for cc in range(2):
                     ip[k, cc, s * X + xx] = part[xx, cc]
             remote(ip.at[k, other, pl.ds(s * X, X)], pr.at[k, j], pr_ssem.at[k], pr_rsem.at[k, j], col, partner).start()
+            if j >= lag:
+                item_send(k, j - lag)
 
     def item_parts(k):
         eu = eu_pan[k].reshape(Z * UB, E)
-        item_share(k, lambda s: jnp.dot(adjt[s], eu, preferred_element_type=F32))
+        item_share(k, lambda s: jnp.dot(adjt[s], eu, preferred_element_type=F32), lag=3)
 
     def item_pair(n):
         near = [zat(d) for d in ((0, 1), (-1, 2), (-2, 3), (-3, 4))[n]]
@@ -234,16 +259,20 @@
         else:
             item_share(1, add)
 
-    def item_send(k):
-        for j, dy in enumerate((2, 1, 3, 0)):
-            s = yat(dy)
-            wait_bytes(pr.at[k, j], pr_rsem.at[k, j])
-            iq[k, pl.ds(s * X, X)] = ip[k, c, pl.ds(s * X, X)] + pr[k, j]
-            for dx in (2, 1, 3, 0):
-                if dy or dx:
-                    px = xat(dx)
-                    remote(iq.at[k, s * X + px], ir.at[k, dy * X + dx - 1], ip_ssem.at[k], ip_rsem.at[k],
-                           z * Y + s, px * 2 + c).start()
+    def item_send(k, j):
+        dy = (2, 1, 3, 0)[j]
+        s = yat(dy)
+        wait_bytes(pr.at[k, j], pr_rsem.at[k, j])
+        iq[k, pl.ds(s * X, X)] = ip[k, c, pl.ds(s * X, X)] + pr[k, j]
+        for dx in (2, 1, 3, 0):
+            if dy or dx:
+                px = xat(dx)
+                remote(iq.at[k, s * X + px], ir.at[k, dy * X + dx - 1], ip_ssem.at[k], ip_rsem.at[k],
+                       z * Y + s, px * 2 + c).start()
+
+    def items_send(k, first=0):
+        for j in range(first, Y):
+            item_send(k, j)
 
     def item_total(k):
         wait_bytes(ir.at[k], ip_rsem.at[k])
@@ -311,13 +340,17 @@
                     user_piece(k, 2 * step + 2)
                 else:
                     user_piece(k, 7)
-                for h in range(NH // 2):
-                    for way in range(2):
-                        emit(way, step, early[way][h])
-                if step < 3:
-                    for h in range(NH // 2):
-                        for way in range(2):
-                            emit(way, step + 1, late[way][h])
+                def run(groups):
+                    for ways in groups:
+                        for h in range(NH // 2):
+                            for way in ways:
+                                emit(way, step, early[way][h])
+                        for h in range(NH // 2):
+                            for way in ways:
+                                if step < 3:
+                                    emit(way, step + 1, late[way][h])
+
+                ring_order(step - 1, run)
                 hook('after', step)
         parts = []
         for h in range(NH):
@@ -338,15 +371,12 @@
     def items_wait(k):
         wait_plane(ei_pan.at[k], fw_rsem.at[k])
 
-    def items0():
-        item_parts(0)
-        item_send(0)
-
     hop0(1)
     items_wait(0)
-    new_user = user_total(0, {('piece', 0): lambda: hop0(2), ('piece', 1): last0, ('own',): items0})
+    new_user = user_total(0, {('piece', 0): lambda: hop0(2), ('piece', 1): last0, ('own',): lambda: item_parts(0)})
     begin1, hop1, last1 = gather_user(1)
     begin1(new_user)
+    items_send(0, 1)
     hop1(0)
     item_pair(0)
     hop1(1)
@@ -357,7 +387,7 @@
     last1()
     item_pair(3)
     items_forward(1)
-    item_send(1)
+    items_send(1)
     items_wait(1)
     new_user = user_total(1, {('after', 2): lambda: items_next(1)})
     begin2, hop2, last2 = gather_user(2)
@@ -365,22 +395,23 @@
     items_forward(2)
     items_wait(2)
 
-    user_total(2, {('after', 1): lambda: hop2(0), ('after', 2): lambda: hop2(1), ('after', 3): lambda: hop2(2)})
+    user_total(2, {('after', 1): lambda: hop2(0), ('after', 2): lambda: hop2(1)})
     final_user = (usum[...] / (LAYERS + 1)).astype(BF16)
     fu_v[...] = final_user
-    outs = [pltpu.make_async_copy(fu_v, fu_hbm, out_sem.at[0])]
+    outs = [pltpu.make_async_copy(fu_v, fu_out, out_sem.at[0])]
     outs[0].start()
 
     qs[...] = jnp.dot(hot[...], final_user, preferred_element_type=F32).astype(BF16).reshape(2, G // 2, QB, E)
     to_partner = remote(qs.at[other], qp, q_ssem.at[0], q_rsem.at[0], col, partner)
     to_partner.start()
+    hop2(2)
     to_partner.wait_recv()
     qt[...] = (qs[c].astype(F32) + qp[...].astype(F32)).astype(BF16)
     for slot, dx, py, px in plane():
         remote(qt.at[px * Y + py], qr.at[slot], q_ssem.at[1], q_rsem.at[1], z * Y + py, px * 2 + c).start()
     last2()
     item_parts(2)
-    item_send(2)
+    items_send(2, 1)
     wait_bytes(qr, q_rsem.at[1])
     total = qt[spot].astype(F32)
     for slot in range(G // 2 - 1):
@@ -395,13 +426,13 @@
     gather_plane(qall, q_ssem.at[3], qg_rsem)
     new_item = item_total(2).astype(BF16)
     fi_v[...] = ((isum[...] + new_item.astype(F32)) / (LAYERS + 1)).astype(BF16)
-    outs.append(pltpu.make_async_copy(fi_v, fi_hbm, out_sem.at[1]))
+    outs.append(pltpu.make_async_copy(fi_v, fi_out, out_sem.at[1]))
     outs[1].start()
     forward_plane(qall, qg_rsem, q_ssem.at[4], qf_rsem)
-    outs.append(pltpu.make_async_copy(qall.at[c], q_hbm.at[c], out_sem.at[2]))
+    outs.append(pltpu.make_async_copy(qall.at[c], q_out.at[c], out_sem.at[2]))
     outs[2].start()
     wait_plane(qall, qf_rsem)
-    outs.append(pltpu.make_async_copy(qall.at[other], q_hbm.at[other], out_sem.at[3]))
+    outs.append(pltpu.make_async_copy(qall.at[other], q_out.at[other], out_sem.at[3]))
     outs[3].start()
 
     wait_bytes(rs_y, rs_ssem.at[0])
@@ -433,16 +464,19 @@
 
 def propagate(mask, user, item, queries):
     dma = pltpu.SemaphoreType.DMA
-    vmem, hbm = pl.BlockSpec(memory_space=pltpu.VMEM), pl.BlockSpec(memory_space=pl.ANY)
+    vmem, free = pl.BlockSpec(memory_space=pltpu.VMEM), pl.BlockSpec(memory_space=pl.ANY)
     L, N = LAYERS, G // 2
     final_user, final_item, picked = pl.pallas_call(
         kernel,
         out_shape=(jax.ShapeDtypeStruct((UB, E), BF16), jax.ShapeDtypeStruct((IB, E), BF16),
                    jax.ShapeDtypeStruct((2, N, QB, E), BF16)),
-        in_specs=[hbm, vmem, vmem, vmem],
-        out_specs=(hbm, hbm, hbm),
+        in_specs=[pl.BlockSpec(memory_space=pltpu.HBM)] * 4,
+        out_specs=(free, free, free),
         scratch_shapes=[
             pltpu.VMEM((Z, Y * UB, E), jnp.int32),
+            pltpu.VMEM((UB, E), BF16),
+            pltpu.VMEM((IB, E), BF16),
+            pltpu.VMEM((1, NQ), jnp.int32),
             pltpu.VMEM((Y, Z, UB, E), BF16),
             pltpu.VMEM((Z, Y - 1, UB, E), BF16),
             pltpu.VMEM((Y, Z, UB, E), BF16),
@@ -477,7 +511,7 @@
             pltpu.VMEM((IB, E), BF16),
             pltpu.VMEM((UB, E), F32),
             pltpu.VMEM((IB, E), F32),
-            dma((Z,)), dma, dma((Z,)),
+            dma((Z + 3,)), dma, dma((Z,)),
             dma((2,)), dma, dma,
             dma((2,)), dma((2,)),
             dma((L,)), dma((L, X)), dma((L,)), dma((L, X)),
@@ -487,14 +521,15 @@
             dma((5,)), dma((3,)), dma((X,)), dma((X,)),
             dma((4,)),
         ],
-        compiler_params=pltpu.CompilerParams(collective_id=0, has_side_effects=True, vmem_limit_bytes=60 * 2**20),
-    )(mask, user, item, queries.reshape(1, NQ))
+        compiler_params=pltpu.CompilerParams(collective_id=0, has_side_effects=True, vmem_limit_bytes=50 * 2**20),
+    )(*(pltpu.with_memory_space_constraint(a, pltpu.HBM) for a in (mask, user, item, queries.reshape(1, NQ))))
     final_user, final_item, scores = pl.pallas_call(
         finish,
         out_shape=(jax.ShapeDtypeStruct((UB, E), BF16), jax.ShapeDtypeStruct((IB, E), BF16),
                    jax.ShapeDtypeStruct((IB, NQ), F32)),
         in_specs=[vmem, vmem, vmem],
         out_specs=(vmem, vmem, vmem),
+        compiler_params=pltpu.CompilerParams(vmem_limit_bytes=8 * 2**20),
     )(final_user, final_item, picked.reshape(NQ, E))
     return final_user, final_item, scores.T
 

time: 114 us -> 114 us (level)
  no operation moved by 1% of the time
where the time goes in v7:
time: 114 us
  Pallas kernels  113 us (99%)
    pallas_call x1, Pallas kernels, propagate(): pl.pallas_call(kernel, out_shape=(jax.ShapeDtypeStruct((UB, E), BF16), ja...  113 us

profile of v7, /device:TPU:1, one launch (start us, length us, event | category | flops | bytes accessed | tf_op | source)
XLA Modules:
  0.0 114.1 jit_solution(7486962410701017888)
XLA Ops:
  0.6 112.6 %shard_map.67 = (bf16[128,256]{1,0:T(8,128)(2,1)S(1)}, bf16[32,256]{1,0:T(8,128)(2,1)S(1)}, bf16[2,16,32,256]{3,2,1,0:T(8,128)(2,1)S(1)}) custom-call(s32[4096,256]{1,0:T(8,128)} %mask_ref.1, bf16[128,256]{1,0:T(8,128)(2,1)} %user_hbm.1, bf16[32,256]{1,0:T(8,128)(2,1)} %item_hbm.1, s32[1,1024]{1,0:T(1,128)} %bitcast.4), custom_call_target="tpu_custom_call" | custom-call | tf_op jit(solution)/shard_map/pallas_call | solution.py:469
  113.2 0.9 shard_map.68

commit v8 on v7

--- a/solution.py
+++ b/solution.py
@@ -106,9 +106,6 @@
     for j, d in enumerate(order):
         zc = zat(d)
         loads[j].wait()
-        if j == 1:
-            pl.semaphore_wait(barrier, R - 1 + Y - 1 + Z - 1)
-            send_mask(0)
         for p in range(Y):
             wide = mask_v[j, p * UB:(p + 1) * UB, :].astype(F32)
             block = wide.astype(BF16)
@@ -156,12 +153,14 @@
 
         return begin, hop, last
 
+    pl.semaphore_wait(barrier, R - 1 + Y - 1 + Z - 1)
     for d in range(1, Y):
         remote(rs_send.at[yat(d)], rs_y.at[d - 1], rs_ssem.at[0], rs_rsem, z * Y + yat(d), row).start()
     for d in range(1, R):
         remote(cs_send, cs_row.at[row], cs_ssem.at[0], cs_rsem.at[0], col, lax.rem(row + d, R)).start()
     for d in range(1, Y):
         remote(item_ref, ei_pan.at[0, c, spot], ei_ssem.at[0], ei_rsem.at[0, 0], z * Y + yat(d), row).start()
+    send_mask(0)
     begin0, hop0, last0 = gather_user(0)
     begin0(user_ref[...])
     send_mask(1)

time: 114 us -> 111 us (0.974)
  Pallas kernels: 113 us -> 110 us
    pallas_call x1, Pallas kernels: 113 us -> 109 us  [propagate(): pl.pallas_call(kernel, out_shape=(jax.ShapeDtypeStruct((UB, E), BF16), ja...]
where the time goes in v8:
time: 111 us
  Pallas kernels  110 us (99%)
    pallas_call x1, Pallas kernels, propagate(): pl.pallas_call(kernel, out_shape=(jax.ShapeDtypeStruct((UB, E), BF16), ja...  109 us

profile of v8, /device:TPU:1, one launch (start us, length us, event | category | flops | bytes accessed | tf_op | source)
XLA Modules:
  0.0 110.8 jit_solution(5335671860001803605)
XLA Ops:
  0.6 109.2 %shard_map.67 = (bf16[128,256]{1,0:T(8,128)(2,1)S(1)}, bf16[32,256]{1,0:T(8,128)(2,1)S(1)}, bf16[2,16,32,256]{3,2,1,0:T(8,128)(2,1)S(1)}) custom-call(s32[4096,256]{1,0:T(8,128)} %mask_ref.1, bf16[128,256]{1,0:T(8,128)(2,1)} %user_hbm.1, bf16[32,256]{1,0:T(8,128)(2,1)} %item_hbm.1, s32[1,1024]{1,0:T(1,128)} %bitcast.4), custom_call_target="tpu_custom_call" | custom-call | tf_op jit(solution)/shard_map/pallas_call | solution.py:468
  109.8 0.9 shard_map.68

commit v9 on v8

--- a/solution.py
+++ b/solution.py
@@ -122,7 +122,7 @@
     def gather_user(k):
         def send(way, step, h):
             src = eu_pan.at[k, zat(-step if way == 0 else step), pl.ds(h * H, H)]
-            remote(src, src, ag_ssem.at[k], ag_rsem.at[way, step, h], right if way == 0 else left, row).start()
+            remote(src, src, ag_ssem, ag_rsem.at[way, step, h], right if way == 0 else left, row).start()
 
         def got(way, step, h):
             dst = eu_pan.at[k, zat(-step - 1 if way == 0 else step + 1), pl.ds(h * H, H)]
@@ -159,7 +159,7 @@
     for d in range(1, R):
         remote(cs_send, cs_row.at[row], cs_ssem.at[0], cs_rsem.at[0], col, lax.rem(row + d, R)).start()
     for d in range(1, Y):
-        remote(item_ref, ei_pan.at[0, c, spot], ei_ssem.at[0], ei_rsem.at[0, 0], z * Y + yat(d), row).start()
+        remote(item_ref, ei_pan.at[0, c, spot], ei_ssem, ei_rsem.at[0, 0], z * Y + yat(d), row).start()
     send_mask(0)
     begin0, hop0, last0 = gather_user(0)
     begin0(user_ref[...])
@@ -175,8 +175,8 @@
     wait_bytes(ei_pan.at[0, c, pl.ds(0, Y - 1)], ei_rsem.at[0, 0])
     own = ei_pan.at[0, c, pl.ds(x * Y, Y)]
     for d in range(1, X):
-        remote(own, own, ei_ssem.at[0], ei_rsem.at[0, d], col, xat(d) * 2 + c).start()
-    remote(own, own, fw_ssem.at[0], fw_rsem.at[0, 0], col, partner).start()
+        remote(own, own, ei_ssem, ei_rsem.at[0, d], col, xat(d) * 2 + c).start()
+    remote(own, own, fw_ssem, fw_rsem.at[0, 0], col, partner).start()
 
     wait_bytes(cs_row.at[pl.ds(0, R - 1)], cs_rsem.at[0])
     deg = cs_row[0]
@@ -196,7 +196,7 @@
     for d in (1, 3, 2):
         rows = pl.ds(xat(-d) * Y, Y)
         wait_bytes(ei_pan.at[0, c, rows], ei_rsem.at[0, d])
-        remote(ei_pan.at[0, c, rows], ei_pan.at[0, c, rows], fw_ssem.at[0], fw_rsem.at[0, d], col, partner).start()
+        remote(ei_pan.at[0, c, rows], ei_pan.at[0, c, rows], fw_ssem, fw_rsem.at[0, d], col, partner).start()
     wait_bytes(cs_y.at[pl.ds(0, Y - 1)], cs_rsem.at[1])
     for s in range(Y):
         invi[s] = lax.rsqrt(jnp.maximum(cs_y[s], 1.0))
@@ -235,7 +235,7 @@
             for xx in range(X):
                 for cc in range(2):
                     ip[k, cc, s * X + xx] = part[xx, cc]
-            remote(ip.at[k, other, pl.ds(s * X, X)], pr.at[k, j], pr_ssem.at[k], pr_rsem.at[k, j], col, partner).start()
+            remote(ip.at[k, other, pl.ds(s * X, X)], pr.at[k, j], pr_ssem, pr_rsem.at[k % 2, j], col, partner).start()
             if j >= lag:
                 item_send(k, j - lag)
 
@@ -243,9 +243,11 @@
         eu = eu_pan[k].reshape(Z * UB, E)
         item_share(k, lambda s: jnp.dot(adjt[s], eu, preferred_element_type=F32), lag=3)
 
-    def item_pair(n):
-        near = [zat(d) for d in ((0, 1), (-1, 2), (-2, 3), (-3, 4))[n]]
-        eu = jnp.concatenate([eu_pan[1, zc] for zc in near], axis=0)
+    pairs = (((4, 3), (-3, 2), (-2, 1), (-1, 0)), ((0, 1), (-1, 2), (-2, 3), (-3, 4)))
+
+    def item_pair(k, n):
+        near = [zat(d) for d in pairs[k][n]]
+        eu = jnp.concatenate([eu_pan[k, zc] for zc in near], axis=0)
 
         def add(s):
             lhs = jnp.concatenate([adjt[s, :, pl.ds(pl.multiple_of(zc * UB, UB), UB)] for zc in near], axis=1)
@@ -256,17 +258,17 @@
             for s in range(Y):
                 macc[s] = add(s)
         else:
-            item_share(1, add)
+            item_share(k, add)
 
     def item_send(k, j):
         dy = (2, 1, 3, 0)[j]
         s = yat(dy)
-        wait_bytes(pr.at[k, j], pr_rsem.at[k, j])
+        wait_bytes(pr.at[k, j], pr_rsem.at[k % 2, j])
         iq[k, pl.ds(s * X, X)] = ip[k, c, pl.ds(s * X, X)] + pr[k, j]
         for dx in (2, 1, 3, 0):
             if dy or dx:
                 px = xat(dx)
-                remote(iq.at[k, s * X + px], ir.at[k, dy * X + dx - 1], ip_ssem.at[k], ip_rsem.at[k],
+                remote(iq.at[k, s * X + px], ir.at[k, dy * X + dx - 1], ip_ssem, ip_rsem.at[k],
                        z * Y + s, px * 2 + c).start()
 
     def items_send(k, first=0):
@@ -284,11 +286,11 @@
         for slot, dx, py, px in plane():
             remote(pan.at[c, spot], pan.at[c, spot], ssem, rsem.at[dx], z * Y + py, px * 2 + c).start()
 
-    def forward_plane(pan, rsem, fssem, frsem):
+    def forward_plane(pan, rsem, fssem, frsem, dst):
         for dx in (0, 1, 3, 2):
             rows = pl.ds(xat(-dx) * Y, Y)
             wait_bytes(pan.at[c, pl.ds(0, Y if dx else Y - 1)], rsem.at[dx])
-            remote(pan.at[c, rows], pan.at[c, rows], fssem, frsem.at[dx], col, partner).start()
+            remote(pan.at[c, rows], dst.at[c, rows], fssem, frsem.at[dx], col, partner).start()
 
     def wait_plane(pan, frsem):
         for dx in (0, 1, 3, 2):
@@ -362,29 +364,38 @@
         new_item = item_total(k).astype(BF16)
         isum[...] += new_item.astype(F32)
         ei_pan[k + 1, c, spot] = new_item
-        gather_plane(ei_pan.at[k + 1], ei_ssem.at[k + 1], ei_rsem.at[k + 1])
+        gather_plane(ei_pan.at[k + 1], ei_ssem, ei_rsem.at[(k + 1) % 2])
 
     def items_forward(k):
-        forward_plane(ei_pan.at[k], ei_rsem.at[k], fw_ssem.at[k], fw_rsem.at[k])
+        forward_plane(ei_pan.at[k], ei_rsem.at[k % 2], fw_ssem, fw_rsem.at[k % 2], ei_pan.at[k])
 
     def items_wait(k):
-        wait_plane(ei_pan.at[k], fw_rsem.at[k])
+        wait_plane(ei_pan.at[k], fw_rsem.at[k % 2])
 
     hop0(1)
     items_wait(0)
-    new_user = user_total(0, {('piece', 0): lambda: hop0(2), ('piece', 1): last0, ('own',): lambda: item_parts(0)})
+
+    def first_pair():
+        last0()
+        item_pair(0, 0)
+
+    def last_pair():
+        item_pair(0, 3)
+        items_send(0)
+
+    new_user = user_total(0, {('piece', 0): lambda: hop0(2), ('piece', 1): first_pair, ('piece', 2): lambda: item_pair(0, 1),
+                              ('piece', 3): lambda: item_pair(0, 2), ('own',): last_pair})
     begin1, hop1, last1 = gather_user(1)
     begin1(new_user)
-    items_send(0, 1)
     hop1(0)
-    item_pair(0)
+    item_pair(1, 0)
     hop1(1)
-    item_pair(1)
+    item_pair(1, 1)
     items_next(0)
     hop1(2)
-    item_pair(2)
+    item_pair(1, 2)
     last1()
-    item_pair(3)
+    item_pair(1, 3)
     items_forward(1)
     items_send(1)
     items_wait(1)
@@ -427,25 +438,23 @@
     fi_v[...] = ((isum[...] + new_item.astype(F32)) / (LAYERS + 1)).astype(BF16)
     outs.append(pltpu.make_async_copy(fi_v, fi_out, out_sem.at[1]))
     outs[1].start()
-    forward_plane(qall, qg_rsem, q_ssem.at[4], qf_rsem)
+    forward_plane(qall, qg_rsem, q_ssem.at[4], qf_rsem, q_out)
     outs.append(pltpu.make_async_copy(qall.at[c], q_out.at[c], out_sem.at[2]))
     outs[2].start()
-    wait_plane(qall, qf_rsem)
-    outs.append(pltpu.make_async_copy(qall.at[other], q_out.at[other], out_sem.at[3]))
-    outs[3].start()
+    wait_plane(q_out, qf_rsem)
 
     wait_bytes(rs_y, rs_ssem.at[0])
     wait_bytes(rs_z.at[pl.ds(0, Z - 1)], rs_ssem.at[1])
     wait_bytes(cs_row.at[pl.ds(0, R - 1)], cs_ssem.at[0])
     wait_bytes(cs_y.at[pl.ds(0, Y - 1)], cs_ssem.at[1])
     wait_bytes(msend.at[pl.ds(0, Y - 1)], mask_ssem)
+    wait_bytes(ei_pan.at[:, 0, pl.ds(0, G // 2 - 1)], ei_ssem)
+    wait_bytes(ei_pan.at[:, 0], fw_ssem)
+    wait_bytes(pr, pr_ssem)
+    wait_bytes(ir, ip_ssem)
+    wait_bytes(eu_pan.at[:, pl.ds(0, 7)], ag_ssem)
     for k in range(LAYERS):
-        wait_bytes(ei_pan.at[k, 0, pl.ds(0, G // 2 - 1)], ei_ssem.at[k])
-        wait_bytes(ei_pan.at[k, 0], fw_ssem.at[k])
-        wait_bytes(pr.at[k], pr_ssem.at[k])
-        wait_bytes(ir.at[k], ip_ssem.at[k])
         wait_bytes(up.at[pl.ds(0, 7)], us_ssem.at[k])
-        wait_bytes(eu_pan.at[k, pl.ds(0, 7)], ag_ssem.at[k])
     to_partner.wait_send()
     wait_bytes(qr, q_ssem.at[1])
     wait_bytes(qz, q_ssem.at[2])
@@ -513,12 +522,12 @@
             dma((Z + 3,)), dma, dma((Z,)),
             dma((2,)), dma, dma,
             dma((2,)), dma((2,)),
-            dma((L,)), dma((L, X)), dma((L,)), dma((L, X)),
+            dma, dma((2, X)), dma, dma((2, X)),
             dma((L,)), dma((2, 4, NH)),
-            dma((L,)), dma((L, Y)), dma((L,)), dma((L,)),
-            dma((L,)), dma((2, 4, NH)),
+            dma, dma((2, Y)), dma, dma((L,)),
+            dma, dma((2, 4, NH)),
             dma((5,)), dma((3,)), dma((X,)), dma((X,)),
-            dma((4,)),
+            dma((3,)),
         ],
         compiler_params=pltpu.CompilerParams(collective_id=0, has_side_effects=True, vmem_limit_bytes=50 * 2**20),
     )(*(pltpu.with_memory_space_constraint(a, pltpu.HBM) for a in (mask, user, item, queries.reshape(1, NQ))))

time: 111 us -> 112 us (level)
    pallas_call x1, Pallas kernels: 109 us -> 110 us  [propagate(): pl.pallas_call(kernel, out_shape=(jax.ShapeDtypeStruct((UB, E), BF16), ja...]
where the time goes in v9:
time: 112 us
  Pallas kernels  111 us (99%)
    pallas_call x1, Pallas kernels, propagate(): pl.pallas_call(kernel, out_shape=(jax.ShapeDtypeStruct((UB, E), BF16), ja...  110 us

profile of v9, /device:TPU:1, one launch (start us, length us, event | category | flops | bytes accessed | tf_op | source)
XLA Modules:
  0.0 111.9 jit_solution(8849208825030180314)
XLA Ops:
  0.6 110.3 %shard_map.67 = (bf16[128,256]{1,0:T(8,128)(2,1)S(1)}, bf16[32,256]{1,0:T(8,128)(2,1)S(1)}, bf16[2,16,32,256]{3,2,1,0:T(8,128)(2,1)S(1)}) custom-call(s32[4096,256]{1,0:T(8,128)} %mask_ref.1, bf16[128,256]{1,0:T(8,128)(2,1)} %user_hbm.1, bf16[32,256]{1,0:T(8,128)(2,1)} %item_hbm.1, s32[1,1024]{1,0:T(1,128)} %bitcast.4), custom_call_target="tpu_custom_call" | custom-call | tf_op jit(solution)/shard_map/pallas_call | solution.py:477
  111.0 0.9 shard_map.68

commit v10 on v9

--- a/solution.py
+++ b/solution.py
@@ -375,18 +375,10 @@
     hop0(1)
     items_wait(0)
 
-    def first_pair():
-        last0()
-        item_pair(0, 0)
-
-    def last_pair():
-        item_pair(0, 3)
-        items_send(0)
-
-    new_user = user_total(0, {('piece', 0): lambda: hop0(2), ('piece', 1): first_pair, ('piece', 2): lambda: item_pair(0, 1),
-                              ('piece', 3): lambda: item_pair(0, 2), ('own',): last_pair})
+    new_user = user_total(0, {('piece', 0): lambda: hop0(2), ('piece', 1): last0, ('own',): lambda: item_parts(0)})
     begin1, hop1, last1 = gather_user(1)
     begin1(new_user)
+    items_send(0, 1)
     hop1(0)
     item_pair(1, 0)
     hop1(1)
@@ -405,7 +397,7 @@
     items_forward(2)
     items_wait(2)
 
-    user_total(2, {('after', 1): lambda: hop2(0), ('after', 2): lambda: hop2(1)})
+    user_total(2, {('after', 2): lambda: hop2(0), ('after', 3): lambda: hop2(1)})
     final_user = (usum[...] / (LAYERS + 1)).astype(BF16)
     fu_v[...] = final_user
     outs = [pltpu.make_async_copy(fu_v, fu_out, out_sem.at[0])]

time: 112 us -> 110 us (0.982)
    pallas_call x1, Pallas kernels: 110 us -> 109 us  [propagate(): pl.pallas_call(kernel, out_shape=(jax.ShapeDtypeStruct((UB, E), BF16), ja...]
where the time goes in v10:
time: 110 us
  Pallas kernels  110 us (100%)
    pallas_call x1, Pallas kernels, propagate(): pl.pallas_call(kernel, out_shape=(jax.ShapeDtypeStruct((UB, E), BF16), ja...  109 us

profile of v10, /device:TPU:1, one launch (start us, length us, event | category | flops | bytes accessed | tf_op | source)
XLA Modules:
  0.0 110.2 jit_solution(15524848044727852540)
XLA Ops:
  0.6 108.6 %shard_map.67 = (bf16[128,256]{1,0:T(8,128)(2,1)S(1)}, bf16[32,256]{1,0:T(8,128)(2,1)S(1)}, bf16[2,16,32,256]{3,2,1,0:T(8,128)(2,1)S(1)}) custom-call(s32[4096,256]{1,0:T(8,128)} %mask_ref.1, bf16[128,256]{1,0:T(8,128)(2,1)} %user_hbm.1, bf16[32,256]{1,0:T(8,128)(2,1)} %item_hbm.1, s32[1,1024]{1,0:T(1,128)} %bitcast.4), custom_call_target="tpu_custom_call" | custom-call | tf_op jit(solution)/shard_map/pallas_call | solution.py:469
  109.2 0.9 shard_map.68

commit v11 on v10

--- a/solution.py
+++ b/solution.py
@@ -99,7 +99,7 @@
     colsum = jnp.zeros((8, E), F32)
 
     def send_mask(j):
-        for d in range(1, Y):
+        for d in (2, 1, 3):
             py = yat(d)
             remote(msend.at[py, j], mrecv.at[j, d - 1], mask_ssem, mask_rsem.at[j], z * Y + py, row).start()
 
@@ -419,8 +419,10 @@
     for slot in range(G // 2 - 1):
         total = total + qr[slot].astype(F32)
     qzs[...] = total.astype(BF16)
-    for d in (4, 3, 5, 2, 6, 1, 7):
-        remote(qzs, qz.at[d - 1], q_ssem.at[2], q_rsem.at[2], zat(d) * Y + y, row).start()
+    for t in (0, 1, 7, 2, 6, 3, 5, 4):
+        def to_plane(t=t):
+            remote(qzs, qz.at[lax.rem(t - z + Z, Z) - 1], q_ssem.at[2], q_rsem.at[2], t * Y + y, row).start()
+        pl.when(z != t)(to_plane)
     wait_bytes(qz, q_rsem.at[2])
     for d in range(Z - 1):
         total = total + qz[d].astype(F32)

time: 110 us -> 110 us (level)
  no operation moved by 1% of the time
where the time goes in v11:
time: 110 us
  Pallas kernels  109 us (99%)
    pallas_call x1, Pallas kernels, propagate(): pl.pallas_call(kernel, out_shape=(jax.ShapeDtypeStruct((UB, E), BF16), ja...  108 us

profile of v11, /device:TPU:1, one launch (start us, length us, event | category | flops | bytes accessed | tf_op | source)
XLA Modules:
  0.0 109.7 jit_solution(3371455119482633656)
XLA Ops:
  0.6 108.2 %shard_map.67 = (bf16[128,256]{1,0:T(8,128)(2,1)S(1)}, bf16[32,256]{1,0:T(8,128)(2,1)S(1)}, bf16[2,16,32,256]{3,2,1,0:T(8,128)(2,1)S(1)}) custom-call(s32[4096,256]{1,0:T(8,128)} %mask_ref.1, bf16[128,256]{1,0:T(8,128)(2,1)} %user_hbm.1, bf16[32,256]{1,0:T(8,128)(2,1)} %item_hbm.1, s32[1,1024]{1,0:T(1,128)} %bitcast.4), custom_call_target="tpu_custom_call" | custom-call | tf_op jit(solution)/shard_map/pallas_call | solution.py:471
  108.8 0.9 shard_map.68

commit v12 on v11

--- a/solution.py
+++ b/solution.py
@@ -375,10 +375,9 @@
     hop0(1)
     items_wait(0)
 
-    new_user = user_total(0, {('piece', 0): lambda: hop0(2), ('piece', 1): last0, ('own',): lambda: item_parts(0)})
+    new_user = user_total(0, {('piece', 0): lambda: hop0(2), ('piece', 1): last0, ('own',): lambda: (item_parts(0), items_send(0, 1))})
     begin1, hop1, last1 = gather_user(1)
     begin1(new_user)
-    items_send(0, 1)
     hop1(0)
     item_pair(1, 0)
     hop1(1)

time: 110 us -> 110 us (level)
  no operation moved by 1% of the time
where the time goes in v12:
time: 110 us
  Pallas kernels  109 us (99%)
    pallas_call x1, Pallas kernels, propagate(): pl.pallas_call(kernel, out_shape=(jax.ShapeDtypeStruct((UB, E), BF16), ja...  108 us

profile of v12, /device:TPU:1, one launch (start us, length us, event | category | flops | bytes accessed | tf_op | source)
XLA Modules:
  0.0 109.8 jit_solution(16659308922889457587)
XLA Ops:
  0.6 108.2 %shard_map.67 = (bf16[128,256]{1,0:T(8,128)(2,1)S(1)}, bf16[32,256]{1,0:T(8,128)(2,1)S(1)}, bf16[2,16,32,256]{3,2,1,0:T(8,128)(2,1)S(1)}) custom-call(s32[4096,256]{1,0:T(8,128)} %mask_ref.1, bf16[128,256]{1,0:T(8,128)(2,1)} %user_hbm.1, bf16[32,256]{1,0:T(8,128)(2,1)} %item_hbm.1, s32[1,1024]{1,0:T(1,128)} %bitcast.4), custom_call_target="tpu_custom_call" | custom-call | tf_op jit(solution)/shard_map/pallas_call | solution.py:470
  108.9 0.9 shard_map.68
